TPU v7x, 8 devices: a whole 2x2x1 slice. The times are simulated.
8 devices in a mesh: fsdp: 8 (over z, y, x, core).
Axes of the slice: x: 2, y: 2, z: 1, core: 2. Of those that a mesh axis runs over, the one named last changes fastest.
Arguments:
- tokens: int32 [1024, 2], P('fsdp')
- positions: int32 [1024], P('fsdp')
- src_len: int32 [1024], P('fsdp')
- self_k: bfloat16 [2, 1024, 64, 12, 64], P(None, 'fsdp')
- self_v: bfloat16 [2, 1024, 64, 12, 64], P(None, 'fsdp')
- cross_k: bfloat16 [2, 1024, 32, 12, 64], P(None, 'fsdp')
- cross_v: bfloat16 [2, 1024, 32, 12, 64], P(None, 'fsdp')
- attn_w: bfloat16 [2, 6, 768, 768], P(None, None, 'fsdp')
- attn_b: bfloat16 [2, 6, 768], P(None, None, 'fsdp')
- fc1_w: bfloat16 [2, 768, 3072], P(None, 'fsdp')
- fc1_b: bfloat16 [2, 3072], P(None, 'fsdp')
- fc2_w: bfloat16 [2, 3072, 768], P(None, 'fsdp')
- fc2_b: bfloat16 [2, 768], P(None, 'fsdp')
- ln_gain: bfloat16 [2, 3, 768], P(None, None, 'fsdp')
- ln_bias: bfloat16 [2, 3, 768], P(None, None, 'fsdp')
- tok_embed: bfloat16 [50048, 768], P('fsdp')
- pos_embed: bfloat16 [1026, 768], replicated
- emb_norm: bfloat16 [2, 768], replicated
- logit_bias: float32 [50048], P('fsdp')
Outputs:
- output 1: float32 [2, 1024, 50048], P(None, None, 'fsdp')
- output 2: bfloat16 [2, 1024, 64, 12, 64], P(None, 'fsdp')
- output 3: bfloat16 [2, 1024, 64, 12, 64], P(None, 'fsdp')
All inputs are finite; a program needn't handle non-finite values.
Results may differ from a plain program's by a relative error of at most 0.0131539.
Values are sent between devices in bfloat16 or wider.
A program may use at most 1 GiB of HBM per device.

v0:
```python
import jax
import jax.numpy as jnp
from jax import lax
from jax.sharding import PartitionSpec as P, NamedSharding

LN_EPS = 1e-5


def layer_norm(values, gain_row, shift_row):
    row_mean = values.mean(-1, keepdims=True)
    centered = values - row_mean
    variance = (centered * centered).mean(-1, keepdims=True)
    return centered * lax.rsqrt(variance + LN_EPS) * gain_row.astype(jnp.float32) + shift_row.astype(jnp.float32)


def attend(query_rows, key_rows, val_rows, valid_len):
    scores = jnp.einsum('bhd,bthd->bht', query_rows, key_rows, preferred_element_type=jnp.float32)
    valid_mask = jnp.arange(key_rows.shape[1])[None, None, :] < valid_len[:, None, None]
    scores = jnp.where(valid_mask, scores, -jnp.inf)
    weights = jnp.exp(scores - scores.max(-1, keepdims=True))
    mixed_rows = jnp.einsum('bht,bthd->bhd', weights.astype(jnp.bfloat16), val_rows, preferred_element_type=jnp.float32)
    return mixed_rows / weights.sum(-1)[:, :, None]


def project(act_rows, weight, bias_row):
    return jnp.dot(act_rows, weight, preferred_element_type=jnp.float32) + bias_row.astype(jnp.float32)


def decoder_layer(hidden, step_pos, src_len, cache_k, cache_v, cross_k, cross_v, layer_w, layer_b, up_w, up_b, down_w, down_b, ln_gains, ln_shifts):
    num_rows, num_times, num_heads, head_dim = cache_k.shape
    attn_scale = head_dim ** -0.5
    act_rows = hidden.astype(jnp.bfloat16)
    qkv_rows = jnp.einsum('bd,sde->sbe', act_rows, layer_w[:3], preferred_element_type=jnp.float32) + layer_b[:3, None, :].astype(jnp.float32)
    self_query = (qkv_rows[0] * attn_scale).astype(jnp.bfloat16).reshape(num_rows, num_heads, head_dim)
    new_key = qkv_rows[1].astype(jnp.bfloat16).reshape(num_rows, 1, num_heads, head_dim)
    new_val = qkv_rows[2].astype(jnp.bfloat16).reshape(num_rows, 1, num_heads, head_dim)
    write_mask = (jnp.arange(num_times)[None, :] == step_pos[:, None])[:, :, None, None]
    cache_k = jnp.where(write_mask, new_key, cache_k)
    cache_v = jnp.where(write_mask, new_val, cache_v)
    mixed_rows = attend(self_query, cache_k, cache_v, step_pos + 1)
    attn_out = project(mixed_rows.reshape(num_rows, -1).astype(jnp.bfloat16), layer_w[3], layer_b[3])
    hidden = layer_norm(hidden + attn_out, ln_gains[0], ln_shifts[0])
    cross_query = (project(hidden.astype(jnp.bfloat16), layer_w[4], layer_b[4]) * attn_scale).astype(jnp.bfloat16).reshape(num_rows, num_heads, head_dim)
    mixed_rows = attend(cross_query, cross_k, cross_v, src_len)
    cross_out = project(mixed_rows.reshape(num_rows, -1).astype(jnp.bfloat16), layer_w[5], layer_b[5])
    hidden = layer_norm(hidden + cross_out, ln_gains[1], ln_shifts[1])
    inner_act = jax.nn.gelu(project(hidden.astype(jnp.bfloat16), up_w, up_b), approximate=False).astype(jnp.bfloat16)
    hidden = layer_norm(hidden + project(inner_act, down_w, down_b), ln_gains[2], ln_shifts[2])
    return hidden, cache_k, cache_v


def solution(mesh):
    cache_spec = P(None, 'fsdp')
    in_specs = (P('fsdp'), P('fsdp'), P('fsdp'), cache_spec, cache_spec, cache_spec, cache_spec,
                P(None, None, 'fsdp'), P(None, None, 'fsdp'), P(None, 'fsdp'), P(None, 'fsdp'),
                P(None, 'fsdp'), P(None, 'fsdp'), P(None, None, 'fsdp'), P(None, None, 'fsdp'),
                P('fsdp'), P(), P(), P('fsdp'))
    out_specs = (P(None, None, 'fsdp'), cache_spec, cache_spec)

    def local_decode(tokens, positions, src_len, self_k, self_v, cross_k, cross_v, attn_w, attn_b, fc1_w, fc1_b, fc2_w, fc2_b, ln_gain, ln_bias, tok_embed, pos_embed, emb_norm, logit_bias):
        shard_idx = lax.axis_index('fsdp')
        num_layers = attn_w.shape[0]
        num_steps = tokens.shape[1]
        vocab_local = tok_embed.shape[0]
        all_tokens = lax.all_gather(tokens, 'fsdp', axis=0, tiled=True)
        local_ids = all_tokens - shard_idx * vocab_local
        owned_mask = (local_ids >= 0) & (local_ids < vocab_local)
        picked = jnp.take(tok_embed, jnp.clip(local_ids, 0, vocab_local - 1), axis=0)
        picked = jnp.where(owned_mask[:, :, None], picked, jnp.zeros_like(picked))
        tok_rows = lax.psum_scatter(picked, 'fsdp', scatter_dimension=0, tiled=True)
        cache_k = [self_k[layer_idx] for layer_idx in range(num_layers)]
        cache_v = [self_v[layer_idx] for layer_idx in range(num_layers)]
        step_logits = []
        for step_idx in range(num_steps):
            step_pos = positions + step_idx
            start_rows = tok_rows[:, step_idx].astype(jnp.float32) + jnp.take(pos_embed, step_pos + 2, axis=0).astype(jnp.float32)
            hidden = layer_norm(start_rows, emb_norm[0], emb_norm[1])
            for layer_idx in range(num_layers):
                layer_w = lax.all_gather(attn_w[layer_idx], 'fsdp', axis=1, tiled=True)
                layer_b = lax.all_gather(attn_b[layer_idx], 'fsdp', axis=1, tiled=True)
                up_w = lax.all_gather(fc1_w[layer_idx], 'fsdp', axis=0, tiled=True)
                up_b = lax.all_gather(fc1_b[layer_idx], 'fsdp', axis=0, tiled=True)
                down_w = lax.all_gather(fc2_w[layer_idx], 'fsdp', axis=0, tiled=True)
                down_b = lax.all_gather(fc2_b[layer_idx], 'fsdp', axis=0, tiled=True)
                ln_gains = lax.all_gather(ln_gain[layer_idx], 'fsdp', axis=1, tiled=True)
                ln_shifts = lax.all_gather(ln_bias[layer_idx], 'fsdp', axis=1, tiled=True)
                hidden, cache_k[layer_idx], cache_v[layer_idx] = decoder_layer(
                    hidden, step_pos, src_len, cache_k[layer_idx], cache_v[layer_idx], cross_k[layer_idx], cross_v[layer_idx],
                    layer_w, layer_b, up_w, up_b, down_w, down_b, ln_gains, ln_shifts)
            all_rows = lax.all_gather(hidden.astype(jnp.bfloat16), 'fsdp', axis=0, tiled=True)
            logits = jnp.einsum('bd,vd->bv', all_rows, tok_embed, preferred_element_type=jnp.float32) + logit_bias
            step_logits.append(logits)
        return jnp.stack(step_logits), jnp.stack(cache_k), jnp.stack(cache_v)

    return jax.shard_map(local_decode, mesh=mesh, in_specs=in_specs, out_specs=out_specs, check_vma=False)
```

profile of v0, /device:TPU:0, one launch (start us, length us, event | category | flops | bytes accessed | tf_op | source)
XLA Modules:
  0.0 544.8 jit_solution(13635310018841455628)
XLA Ops:
  7.2 13.7 %all_gather.73 = s32[1024,2]{0,1:T(2,128)S(1)} all-gather(s32[128,2]{0,1:T(2,128)} %param.21), channel_id=1, replica_groups=mesh['fsdp'=8] {'fsdp'}, dimensions={0}, use_global_device_ids=true | all-gather | bytes 9216 | tf_op jit(solution)/shard_map/all_gather | solution.py:65
  21.5 15.0 %gather_fusion = bf16[2048,768]{1,0:T(8,128)(2,1)} fusion(bf16[6256,768]{1,0:T(8,128)(2,1)} %param.36, s32[2048]{0:T(1024)S(1)} %broadcast_clamp_fusion), kind=kCustom, calls=%fused_computation.2 | custom fusion | bytes 6299648 | tf_op jit(solution)/shard_map/jit(_take)/gather | solution.py:68
  56.8 22.6 %all-reduce.2 = (bf16[768]{0:T(1024)(128)(2,1)S(1)}, bf16[768]{0:T(1024)(128)(2,1)S(1)}) all-reduce(bf16[768]{0:T(1024)(128)(2,1)S(1)} %dynamic-update-slice, bf16[768]{0:T(1024)(128)(2,1)S(1)} %dynamic-update-slice.1), channel_id=9, replica_groups=mesh['fsdp'=8] {'fsdp'}, use_global_device_ids=true, to_apply=%add | all-reduce | flops 1536 | bytes 6144
  80.1 11.6 %all-gather.5 = bf16[1,3072]{1,0:T(2,128)(2,1)S(1)} all-gather(bf16[1,384]{1,0:T(2,128)(2,1)S(1)} %get-tuple-element.97), channel_id=7, replica_groups=mesh['fsdp'=8] {'fsdp'}, dimensions={1}, use_global_device_ids=true | all-gather | bytes 6912 | tf_op jit(solution)/shard_map/all_gather | solution.py:82
  91.8 10.9 %all-gather.13 = bf16[1,3072]{1,0:T(2,128)(2,1)S(1)} all-gather(bf16[1,384]{1,0:T(2,128)(2,1)S(1)} %get-tuple-element.98), channel_id=15, replica_groups=mesh['fsdp'=8] {'fsdp'}, dimensions={1}, use_global_device_ids=true | all-gather | bytes 6912 | tf_op jit(solution)/shard_map/all_gather | solution.py:82
  105.8 14.6 %all-gather.9 = bf16[1,6,768]{1,0,2:T(2,128)(2,1)S(1)} all-gather(bf16[1,6,96]{1,0,2:T(2,128)(2,1)S(1)} %copy.274), channel_id=11, replica_groups=mesh['fsdp'=8] {'fsdp'}, dimensions={2}, use_global_device_ids=true | all-gather | bytes 10368 | tf_op jit(solution)/shard_map/all_gather | solution.py:80
  120.5 9.8 %fusion.303 = (f32[768]{0:T(1024)}, f32[768]{0:T(1024)}, f32[768]{0:T(1024)}) fusion(bf16[1,6,768]{1,0,2:T(2,128)(2,1)S(1)} %all-gather.9), kind=kLoop, calls=%fused_computation.355 | loop fusion | flops 2304 | bytes 13824 | tf_op jit(solution)/shard_map/add | solution.py:26
  130.7 12.3 %all-gather.1 = bf16[1,6,768]{1,0,2:T(2,128)(2,1)S(1)} all-gather(bf16[1,6,96]{1,0,2:T(2,128)(2,1)S(1)} %copy.270), channel_id=3, replica_groups=mesh['fsdp'=8] {'fsdp'}, dimensions={2}, use_global_device_ids=true | all-gather | bytes 10368 | tf_op jit(solution)/shard_map/all_gather | solution.py:80
  143.0 9.3 %fusion.313 = (f32[768]{0:T(1024)S(1)}, f32[768]{0:T(1024)S(1)}, f32[768]{0:T(1024)S(1)}) fusion(bf16[1,6,768]{1,0,2:T(2,128)(2,1)S(1)} %all-gather.1), kind=kLoop, calls=%fused_computation.375 | loop fusion | flops 2304 | bytes 13824 | tf_op jit(solution)/shard_map/add | solution.py:26
  152.7 15.7 %all-gather.2 = bf16[1,3,768]{1,0,2:T(2,128)(2,1)S(1)} all-gather(bf16[1,3,96]{1,0,2:T(2,128)(2,1)S(1)} %copy.272), channel_id=4, replica_groups=mesh['fsdp'=8] {'fsdp'}, dimensions={2}, use_global_device_ids=true | all-gather | bytes 5184 | tf_op jit(solution)/shard_map/all_gather | solution.py:85
  176.2 13.2 %all-gather.3 = bf16[1,3,768]{1,0,2:T(2,128)(2,1)S(1)} all-gather(bf16[1,3,96]{1,0,2:T(2,128)(2,1)S(1)} %copy.273), channel_id=5, replica_groups=mesh['fsdp'=8] {'fsdp'}, dimensions={2}, use_global_device_ids=true | all-gather | bytes 5184 | tf_op jit(solution)/shard_map/all_gather | solution.py:86
  197.3 13.1 %all-gather.10 = bf16[1,3,768]{1,0,2:T(2,128)(2,1)S(1)} all-gather(bf16[1,3,96]{1,0,2:T(2,128)(2,1)S(1)} %copy.276), channel_id=12, replica_groups=mesh['fsdp'=8] {'fsdp'}, dimensions={2}, use_global_device_ids=true | all-gather | bytes 5184 | tf_op jit(solution)/shard_map/all_gather | solution.py:85
  218.8 13.1 %all-gather.11 = bf16[1,3,768]{1,0,2:T(2,128)(2,1)S(1)} all-gather(bf16[1,3,96]{1,0,2:T(2,128)(2,1)S(1)} %copy.277), channel_id=13, replica_groups=mesh['fsdp'=8] {'fsdp'}, dimensions={2}, use_global_device_ids=true | all-gather | bytes 5184 | tf_op jit(solution)/shard_map/all_gather | solution.py:86
  253.9 12.1 %multiply_reduce_fusion.7 = (f32[128,12,64]{0,1,2:T(8,128)S(1)}, f32[128,12,64]{0,1,2:T(8,128)S(1)}) fusion(f32[128,12,64]{0,2,1:T(8,128)S(1)} %convert.42, bf16[2,128,64,12,64]{1,4,3,2,0:T(8,128)(2,1)} %param.24, pred[128,64]{0,1:T(8,128)(4,1)S(1)} %iota_compare_fusion.2, bf16[128,12,64]{0,2,1:T(8,128)(2,1)S(1)} %bitcast.338, ...), kind=kLoop, calls=%fused_computation.23 | loop fusion | flops 50135040 | bytes 14565376
  267.0 11.0 %multiply_reduce_fusion.6 = (f32[128,12,64]{0,2,1:T(8,128)S(1)}, f32[128,12,64]{0,2,1:T(8,128)S(1)}) fusion(f32[128,12,64]{0,1,2:T(8,128)S(1)} %copy.279, bf16[2,128,64,12,64]{1,4,3,2,0:T(8,128)(2,1)} %param.25, pred[128,64]{0,1:T(8,128)(4,1)S(1)} %iota_compare_fusion.2, bf16[128,12,64]{0,2,1:T(8,128)(2,1)S(1)} %bitcast.336, ...), kind=kLoop, calls=%fused_computation.22 | loop fusion | flops 50135040 | bytes 14565376 | tf_op jit(solution)/shard_map/bht,bthd->bhd/dot_general | solution.py:21
  308.0 8.7 %fusion.602 = (f32[128]{0:T(128)S(1)}, f32[128,768]{1,0:T(8,128)S(1)}) fusion(f32[768]{0:T(1024)S(1)} %convert_element_type.416, bf16[1,3072,768]{2,1,0:T(8,128)(2,1)} %all-gather.33.cloned.1.call-done, bf16[1,768,3072]{2,1,0:T(8,128)(2,1)} %all-gather.31.cloned.1.call-done, f32[3072]{0:T(1024)S(1)} %bitcast.371, f32[128,768]{1,0:T(8,128)S(1)} %get-tuple-element.122, ...), kind=kOutput, calls=%fused_computation.742 | convolution fusion | flops 1235091328 | bytes 10246656 | tf_op jit(solution)/shard_map/dot_general | solution.py:26
  327.4 12.8 %multiply_reduce_fusion.5 = (f32[128,12,64]{0,1,2:T(8,128)S(1)}, f32[128,12,64]{0,1,2:T(8,128)}) fusion(f32[128,12,64]{0,2,1:T(8,128)S(1)} %convert.50, bf16[2,128,64,12,64]{1,4,3,2,0:T(8,128)(2,1)} %param.24, pred[128,64]{0,1:T(8,128)(4,1)S(1)} %copy-done.8, bf16[128,12,64]{0,2,1:T(8,128)(2,1)S(1)} %bitcast.342, bf16[128,12,64]{0,2,1:T(8,128)(2,1)S(1)} %bitcast.340, ...), kind=kLoop, calls=%fused_computation.21 | loop fusion | flops 50135040 | bytes 14565376
  343.1 11.0 %multiply_reduce_fusion.4 = (f32[128,12,64]{0,2,1:T(8,128)S(1)}, f32[128,12,64]{0,2,1:T(8,128)S(1)}) fusion(f32[128,12,64]{0,1,2:T(8,128)S(1)} %copy.283, bf16[2,128,64,12,64]{1,4,3,2,0:T(8,128)(2,1)} %param.25, pred[128,64]{0,1:T(8,128)(4,1)S(1)} %copy-done.8, bf16[128,12,64]{0,2,1:T(8,128)(2,1)S(1)} %bitcast.346, bf16[128,12,64]{0,2,1:T(8,128)(2,1)S(1)} %bitcast.344, ...), kind=kLoop, calls=%fused_computation.20 | loop fusion | flops 50135040 | bytes 14565376 | tf_op jit(solution)/shard_map/bht,bthd->bhd/dot_general | solution.py:21
  398.9 32.4 %select_select_fusion.1 = (bf16[1,128,64,12,64]{1,4,3,2,0:T(8,128)(2,1)}, bf16[1,128,64,12,64]{1,4,3,2,0:T(8,128)(2,1)}, bf16[1,128,64,12,64]{1,4,3,2,0:T(8,128)(2,1)}, bf16[1,128,64,12,64]{1,4,3,2,0:T(8,128)(2,1)}) fusion(pred[128,64]{0,1:T(8,128)(4,1)S(1)} %copy-done.8, pred[128,64]{0,1:T(8,128)(4,1)S(1)} %copy-done.11, ...), kind=kLoop, calls=%fused_computation.45 | loop fusion | flops 50331648 | bytes 102252544 | tf_op jit(solution)/shard_map/jit(_where)/select_n | solution.py:39
  431.4 24.8 %pad_maximum_fusion.2 = bf16[2,128,64,12,64]{1,4,3,2,0:T(8,128)(2,1)} fusion(bf16[1,128,64,12,64]{1,4,3,2,0:T(8,128)(2,1)} %get-tuple-element.53, bf16[1,128,64,12,64]{1,4,3,2,0:T(8,128)(2,1)} %get-tuple-element.52), kind=kLoop, calls=%fused_computation.15 | loop fusion | flops 12582912 | bytes 50331648 | tf_op jit(solution)/shard_map/stack | solution.py:93
  456.2 9.8 %pad_maximum_fusion.1 = bf16[2,128,64,12,64]{1,4,3,2,0:T(8,128)(2,1)} fusion(bf16[1,128,64,12,64]{1,4,3,2,0:T(8,128)(2,1)S(1)} %bitcast.327, bf16[1,128,64,12,64]{1,4,3,2,0:T(8,128)(2,1)S(1)} %bitcast.329), kind=kLoop, calls=%fused_computation.14 | loop fusion | flops 12582912 | bytes 50331648 | tf_op jit(solution)/shard_map/stack | solution.py:93
  466.0 18.6 %add_bitcast_fusion = f32[1,1024,6256]{1,2,0:T(8,128)} fusion(bf16[1024,768]{1,0:T(8,128)(2,1)} %all-gather.27.cloned.1.call-done, bf16[6256,768]{1,0:T(8,128)(2,1)} %param.36, f32[6256]{0:T(1024)S(1)} %copy-done.57), kind=kOutput, calls=%fused_computation.12 | convolution fusion | flops 9846243328 | bytes 36831680 | tf_op jit(solution)/shard_map/bd,vd->bv/dot_general | solution.py:91
  484.6 18.6 %add_bitcast_fusion.1 = f32[1,1024,6256]{1,2,0:T(8,128)} fusion(bf16[1024,768]{1,0:T(8,128)(2,1)} %all-gather.25.cloned.1.call-done, bf16[6256,768]{1,0:T(8,128)(2,1)} %param.36, f32[6256]{0:T(1024)S(1)} %copy-done.57), kind=kOutput, calls=%fused_computation.13 | convolution fusion | flops 9846243328 | bytes 36831680 | tf_op jit(solution)/shard_map/bd,vd->bv/dot_general | solution.py:91
  503.2 34.6 %pad_maximum_fusion = f32[2,1024,6256]{1,2,0:T(8,128)} fusion(f32[1,1024,6256]{1,2,0:T(8,128)} %add_bitcast_fusion, f32[1,1024,6256]{1,2,0:T(8,128)} %add_bitcast_fusion.1), kind=kLoop, calls=%fused_computation.11 | loop fusion | flops 12812288 | bytes 102498304 | tf_op jit(solution)/shard_map/stack | solution.py:93
  (329 shorter events, 159.4 us)
Async XLA Ops:
  7.2 96.9 %copy-start = (bf16[1026,768]{1,0:T(8,128)(2,1)S(1)}, bf16[1026,768]{1,0:T(8,128)(2,1)}, u32[]{:S(2)}) copy-start(bf16[1026,768]{1,0:T(8,128)(2,1)} %param.37) | copy-start | bytes 4727812
  7.2 233.1 %reduce-scatter.2.cloned.1.call-start = ((), (), s32[]{:S(2)}) async-start(), calls=%async_computation.1 | async-start | bytes 3538944 | tf_op jit(solution)/shard_map/reduce_scatter | solution.py:70
  47.7 195.4 %all-gather.29.cloned.1.call-start = ((), (), s32[]{:S(2)}) async-start(), calls=%async_computation.4 | async-start | bytes 7962624 | tf_op jit(solution)/shard_map/all_gather | solution.py:79
  50.5 246.6 %all-gather.31.cloned.1.call-start = ((), (), s32[]{:S(2)}) async-start(), calls=%async_computation.5 | async-start | bytes 5308416 | tf_op jit(solution)/shard_map/all_gather | solution.py:81
  53.0 244.1 %all-gather.33.cloned.1.call-start = ((), (), s32[]{:S(2)}) async-start(), calls=%async_computation.6 | async-start | bytes 5308416 | tf_op jit(solution)/shard_map/all_gather | solution.py:83
  54.2 25.2 %copy-start.32 = (bf16[2,384]{1,0:T(2,128)(2,1)S(1)}, bf16[2,384]{1,0:T(2,128)(2,1)}, u32[]{:S(2)}) copy-start(bf16[2,384]{1,0:T(2,128)(2,1)} %param.31) | copy-start | bytes 4612
  54.2 25.2 %copy-start.33 = (bf16[2,3,96]{2,0,1:T(2,128)(2,1)S(1)}, bf16[2,3,96]{2,0,1:T(2,128)(2,1)}, u32[]{:S(2)}) copy-start(bf16[2,3,96]{2,0,1:T(2,128)(2,1)} %param.34) | copy-start | bytes 3460
  54.2 25.2 %copy-start.34 = (bf16[2,3,96]{2,0,1:T(2,128)(2,1)S(1)}, bf16[2,3,96]{2,0,1:T(2,128)(2,1)}, u32[]{:S(2)}) copy-start(bf16[2,3,96]{2,0,1:T(2,128)(2,1)} %param.35) | copy-start | bytes 3460
  54.2 25.2 %copy-start.56 = (s32[128]{0:T(128)S(1)}, s32[128]{0:T(128)}, u32[]{:S(2)}) copy-start(s32[128]{0:T(128)} %param.23) | copy-start | bytes 1540
  54.2 25.8 %copy-start.31 = (bf16[2,6,96]{2,0,1:T(2,128)(2,1)S(1)}, bf16[2,6,96]{2,0,1:T(2,128)(2,1)}, u32[]{:S(2)}) copy-start(bf16[2,6,96]{2,0,1:T(2,128)(2,1)} %param.29) | copy-start | bytes 6916
  54.2 25.8 %copy-start.29 = (bf16[2,768]{1,0:T(2,128)(2,1)S(1)}, bf16[2,768]{1,0:T(2,128)(2,1)}, u32[]{:S(2)}) copy-start(bf16[2,768]{1,0:T(2,128)(2,1)} %param.38) | copy-start | bytes 9220
  54.2 262.7 %all-gather.35.cloned.1.call-start = ((), (), s32[]{:S(2)}) async-start(), calls=%async_computation.7 | async-start | bytes 7962624 | tf_op jit(solution)/shard_map/all_gather | solution.py:79
  54.8 323.1 %all-gather.37.cloned.1.call-start = ((), (), s32[]{:S(2)}) async-start(), calls=%async_computation.8 | async-start | bytes 5308416 | tf_op jit(solution)/shard_map/all_gather | solution.py:81
  55.4 322.6 %all-gather.39.cloned.1.call-start = ((), (), s32[]{:S(2)}) async-start(), calls=%async_computation.9 | async-start | bytes 5308416 | tf_op jit(solution)/shard_map/all_gather | solution.py:83
  56.2 409.8 %all-gather.27.cloned.1.call-start = ((), (), s32[]{:S(2)}) async-start(), calls=%async_computation.3 | async-start | bytes 1769472 | tf_op jit(solution)/shard_map/all_gather | solution.py:90
  56.3 210.7 %copy-start.7 = (pred[128,64]{0,1:T(8,128)(4,1)}, pred[128,64]{0,1:T(8,128)(4,1)S(1)}, u32[]{:S(2)}) copy-start(pred[128,64]{0,1:T(8,128)(4,1)S(1)} %iota_compare_fusion.2) | copy-start | bytes 24580
  197.3 123.4 %copy-start.12 = (f32[768]{0:T(1024)}, f32[768]{0:T(1024)S(1)}, u32[]{:S(2)}) copy-start(f32[768]{0:T(1024)S(1)} %get-tuple-element.32) | copy-start | bytes 9220
  240.3 25.8 %copy-start.16 = (pred[128,64]{0,1:T(8,128)(4,1)}, pred[128,64]{0,1:T(8,128)(4,1)S(1)}, u32[]{:S(2)}) copy-start(pred[128,64]{0,1:T(8,128)(4,1)S(1)} %get-tuple-element.141) | copy-start | bytes 24580
  240.3 26.2 %copy-start.14 = (pred[128,64]{0,1:T(8,128)(4,1)}, pred[128,64]{0,1:T(8,128)(4,1)S(1)}, u32[]{:S(2)}) copy-start(pred[128,64]{0,1:T(8,128)(4,1)S(1)} %get-tuple-element.103) | copy-start | bytes 24580
  240.3 26.7 %copy-start.9 = (pred[128,64]{0,1:T(8,128)(4,1)}, pred[128,64]{0,1:T(8,128)(4,1)S(1)}, u32[]{:S(2)}) copy-start(pred[128,64]{0,1:T(8,128)(4,1)S(1)} %get-tuple-element.104) | copy-start | bytes 24580
  398.9 85.7 %all-gather.25.cloned.1.call-start = ((), (), s32[]{:S(2)}) async-start(), calls=%async_computation.2 | async-start | bytes 1769472 | tf_op jit(solution)/shard_map/all_gather | solution.py:90
  431.3 24.9 %slice-start = ((s8[12582912]{0:T(1024)(128)(4,1)}), s8[4194304]{0:T(1024)(128)(4,1)S(1)}, s32[]{:S(2)}) async-start(s8[12582912]{0:T(1024)(128)(4,1)} %bitcast.326), calls=%async_computation.10 | async-start | bytes 8388608
  431.3 24.9 %slice-start.3 = ((s8[12582912]{0:T(1024)(128)(4,1)}), s8[4194304]{0:T(1024)(128)(4,1)S(1)}, s32[]{:S(2)}) async-start(s8[12582912]{0:T(1024)(128)(4,1)} %bitcast.328), calls=%async_computation.13 | async-start | bytes 8388608
  503.2 34.6 %copy-start.1 = (bf16[1026,768]{1,0:T(8,128)(2,1)S(1)}, bf16[1026,768]{1,0:T(8,128)(2,1)}, u32[]{:S(2)}) copy-start(bf16[1026,768]{1,0:T(8,128)(2,1)} %param.37) | copy-start | bytes 4727812
  (51 other events, 365.2 us)
Sparse Core Ops, SparseCore 0:
  47.8 37.8 reduce-scatter.1
  88.1 45.4 all-gather.28
  135.4 35.3 all-gather.30
  172.5 35.3 all-gather.32
  210.2 44.7 all-gather.34
  256.7 32.9 all-gather.36
  291.4 33.0 all-gather.38
  399.0 19.7 all-gather.26
  431.4 19.7 all-gather.24
where the time goes:
time: 552 us; the launch traced here: 545 us
  other arithmetic  243 us (44%)
  blocking collectives  141 us (26%)
  matrix products  102 us (18%)
  local copies, waits for them, and re-layouts  40.9 us (7%)
  between operations  16.1 us (3%)
    another operation x3, other arithmetic, local_decode(): return (jnp.stack(step_logits), jnp.stack(cache_k), jnp.stack(cache_v))  69.2 us
    dot_general x16, matrix products, project(): jnp.dot(act_rows, weight, preferred_element_type=jnp.float32)  51.4 us
    unnamed x15, other arithmetic  39.4 us
    dot_general x2, matrix products, local_decode(): jnp.einsum('bd,vd->bv', all_rows, tok_embed, preferred_element_type=jnp.f...  37.1 us
    dot_general x4, other arithmetic, attend(): jnp.einsum('bht,bthd->bhd', weights.astype(jnp.bfloat16), val_rows, prefe...  32.9 us
    select_n x1, other arithmetic, decoder_layer(): cache_v = jnp.where(write_mask, new_val, cache_v)  32.4 us
    all_gather x2, blocking collectives, local_decode(): ln_gains = lax.all_gather(ln_gain[layer_idx], 'fsdp', axis=1, tiled=True)  28.8 us
    all_gather x2, blocking collectives, local_decode(): layer_b = lax.all_gather(attn_b[layer_idx], 'fsdp', axis=1, tiled=True)  27 us
  transfers between devices with their start and end apart: 9, of which 0 were waited for; matrix products, arithmetic and copies ran while one was open for 52% of the time, Pallas kernels for 0%

commit v1 on v0

v1 whole, which is shorter than its diff:
```python
import functools

import jax
import jax.numpy as jnp
from jax import lax
from jax.experimental import pallas as pl
from jax.experimental.pallas import tpu as pltpu
from jax.sharding import PartitionSpec as P


LN_EPS = 1e-5
F32 = jnp.float32
BF16 = jnp.bfloat16
ERF_SCALE = 0.7071067811865476
SLOTS = 16
NONE = {'transcendentals': 0}
MIB = 2 ** 20


def norm_rows(values, gain, shift):
    mean = jnp.mean(values, axis=-1, keepdims=True)
    centered = values - mean
    var = jnp.mean(centered * centered, axis=-1, keepdims=True)
    return centered * lax.rsqrt(var + LN_EPS) * gain.astype(F32) + shift.astype(F32)


def dot32(a, b):
    return jnp.dot(a, b, preferred_element_type=F32)


MESH = pl.DeviceIdType.MESH
VM = pltpu.VMEM
HBM = pl.BlockSpec(memory_space=pltpu.HBM)


def place():
    me = lax.axis_index('fsdp')
    return (me,) + neighbours(me)


def neighbours(me):
    core, x, y = me % 2, (me // 2) % 2, me // 4
    over_x, over_y = 2 * (1 - 2 * x), 4 * (1 - 2 * y)
    first = me + (1 - core) * over_x + core * over_y
    second = me + (1 - core) * over_y + core * over_x
    return me + 1 - 2 * core, first, second


def owners():
    me, pair, first, second = place()
    far = first + second - me
    _, pair_first, pair_second = neighbours(pair)
    return me, first, second, far, pair, pair_first, pair_second, pair_first + pair_second - pair


PAIR = [(i, i ^ 1) for i in range(8)]
FIRST = [(i, i ^ (4 if i % 2 else 2)) for i in range(8)]
SECOND = [(i, i ^ (2 if i % 2 else 4)) for i in range(8)]


def spread(shard):
    def hop(block, pairs):
        return lax.ppermute(block, 'fsdp', pairs)
    a = hop(shard, FIRST)
    b = hop(shard, SECOND)
    ab = hop(a, SECOND)
    mine = [shard, a, b, ab]
    return mine + [hop(m, PAIR) for m in mine]


def rows_of(owner, part):
    return pl.ds(pl.multiple_of(owner * part, part), part)


def load_slot(shards, slot, dst, sems):
    part = shards[0].shape[1]
    return [pltpu.make_async_copy(ref.at[slot], dst.at[rows_of(own, part)], sems.at[i])
            for i, (ref, own) in enumerate(zip(shards, owners()))]


def begin(copies):
    for c in copies:
        c.start()
    return copies


def finish(copies):
    for c in copies:
        c.wait()


def qkv_kernel(layer, x_ref, wide_ref, *rest):
    shards, (out_ref, w, sems) = rest[:8], rest[8:]
    loads = [begin(load_slot(shards, j, w.at[j], sems.at[j])) for j in range(3)]
    x = x_ref[...].astype(BF16)
    for j in range(3):
        finish(loads[j])
        y = dot32(x, w[j]) + bias_row(wide_ref, layer, j)
        if j == 0:
            y = y * 0.125
        out_ref[j] = y.T.astype(BF16)


def small_kernel(*refs):
    srcs, (wide, ids), outs, (ssem, rsem, lsem) = refs[:6], refs[6:8], refs[8:13], refs[13:]
    dsts = list(outs) + [ids]
    me = lax.axis_index('fsdp')
    barrier = pltpu.get_barrier_semaphore()
    for d in range(1, 8):
        pl.semaphore_signal(barrier, inc=1, device_id=((me + d) % 8,), device_id_type=MESH)
    pl.semaphore_wait(barrier, 7)
    sends, own = [], []
    for i in (5, 0, 1, 2, 3, 4):
        for d in range(1, 8):
            c = pltpu.make_async_remote_copy(src_ref=srcs[i], dst_ref=dsts[i].at[me], send_sem=ssem.at[i, d], recv_sem=rsem.at[i, d],
                                             device_id=((me + d) % 8,), device_id_type=MESH)
            c.start()
            sends.append(c)
        c = pltpu.make_async_copy(srcs[i], dsts[i].at[me], lsem.at[i])
        c.start()
        own.append(c)
    for i in range(6):
        for d in range(1, 8):
            slot = dsts[i].at[(me + 8 - d) % 8]
            pltpu.make_async_remote_copy(src_ref=srcs[i], dst_ref=slot, send_sem=ssem.at[i, d], recv_sem=rsem.at[i, d],
                                         device_id=((me + 8 - d) % 8,), device_id_type=MESH).wait_recv()
    for c in sends:
        c.wait_send()
    finish(own)
    at = 0
    for ref in outs[:3]:
        for j in range(ref.shape[1]):
            wide[at:at + 2] = jnp.concatenate([ref[d, j].astype(F32) for d in range(8)], axis=1)
            at += 2
    wide[at:at + 2] = jnp.concatenate([outs[3][d].astype(F32) for d in range(8)], axis=1)
    at += 2
    for j in range(4):
        wide[at:at + 2] = jnp.concatenate([outs[4][d].astype(F32) for d in (2 * j, 2 * j + 1)], axis=1)
        at += 2


def bias_row(wide_ref, layer, slot):
    return wide_ref[pl.ds(2 * slot + layer, 1), :]


def gain_row(wide_ref, layer, norm):
    return wide_ref[pl.ds(12 + 2 * norm + layer, 1), :], wide_ref[pl.ds(18 + 2 * norm + layer, 1), :]


def greet():
    me, pair, first, second = place()
    barrier = pltpu.get_barrier_semaphore()
    for other in (pair, first, second):
        pl.semaphore_signal(barrier, inc=1, device_id=(other,), device_id_type=MESH)
    pl.semaphore_wait(barrier, 3)
    return me, pair, first, second


def embed_kernel(vocab, src, ids, pos_rows, norm_ref, out, r1, s1, r2, s2, r3, ssem, rsem):
    me, pair, first, second = greet()
    core = me % 2

    def send(k, block, dst, device):
        c = pltpu.make_async_remote_copy(src_ref=block, dst_ref=dst, send_sem=ssem.at[k], recv_sem=rsem.at[k],
                                         device_id=(device,), device_id_type=MESH)
        c.start()
        return c
    def chips(at):
        c, cx, cy = at % 2, (at // 2) % 2, at // 4
        flip_x, flip_y = 1 - 2 * cx, 2 * (1 - 2 * cy)
        here = at // 2
        f = here + (1 - c) * flip_x + c * flip_y
        g = here + (1 - c) * flip_y + c * flip_x
        return here, g, f, f + g - here
    def held(block, dest, owner):
        parts = []
        for s in range(ids.shape[1]):
            row = ids[dest, pl.ds(s, 1), :] - owner * vocab
            here = jnp.where((row >= 0) & (row < vocab), 1.0, 0.0)
            tile = jnp.broadcast_to(here, (128, 128)).T.astype(BF16)
            parts.append(block[s * 128:(s + 1) * 128] * jnp.concatenate([tile] * (block.shape[1] // 128), axis=1))
        return jnp.concatenate(parts, axis=0)
    mine = chips(me)
    theirs = chips(pair)
    step = [send(j, src.at[theirs[j] * 2 + (1 - core)], r1.at[j], pair) for j in (2, 3, 1, 0)]
    order = (2, 3, 1, 0)
    hops = {}
    for n, j in enumerate(order):
        step[n].wait()
        dest = mine[j] * 2 + core
        s1[j] = held(src[dest], dest, me) + held(r1[j], dest, pair)
        if j >= 2:
            hops[j] = send(4 + j, s1.at[j], r2.at[j - 2], first)
    for j in (3, 2):
        hops[j].wait()
    s2[...] = s1[1] + r2[1]
    last = send(8, s2, r3, second)
    s1[0] = s1[0] + r2[0]
    last.wait()
    start = (s1[0] + r3[...]).astype(F32) + pos_rows[...].astype(F32)
    out[...] = norm_rows(start, norm_ref[0:1], norm_ref[1:2])


def gather_kernel(src, out, ssem, rsem, lsem):
    me, pair, first, second = greet()
    far = first + second - me
    _, pair_first, pair_second = neighbours(pair)
    pair_far = pair_first + pair_second - pair
    local = pltpu.make_async_copy(src, out.at[me], lsem)
    local.start()

    def send(k, s, block, slot, device):
        c = pltpu.make_async_remote_copy(src_ref=block, dst_ref=out.at[slot, s], send_sem=ssem.at[k, s], recv_sem=rsem.at[k, s],
                                         device_id=(device,), device_id_type=MESH)
        c.start()
        return c

    def arrive(k, s, slot, device):
        pltpu.make_async_remote_copy(src_ref=out.at[slot, s], dst_ref=out.at[slot, s], send_sem=ssem.at[k, s], recv_sem=rsem.at[k, s],
                                     device_id=(device,), device_id_type=MESH).wait_recv()
    sent = []
    halves = range(src.shape[0])
    for s in halves:
        sent.append(send(0, s, src.at[s], me, first))
        sent.append(send(1, s, src.at[s], me, second))
        sent.append(send(3, s, src.at[s], me, pair))
    for s in halves:
        arrive(0, s, first, first)
        sent.append(send(2, s, out.at[first, s], first, second))
        sent.append(send(4, s, out.at[first, s], first, pair))
        arrive(1, s, second, second)
        sent.append(send(5, s, out.at[second, s], second, pair))
    for s in halves:
        arrive(2, s, far, second)
        sent.append(send(6, s, out.at[far, s], far, pair))
    for s in halves:
        arrive(3, s, pair, pair)
        arrive(4, s, pair_first, pair)
        arrive(5, s, pair_second, pair)
        arrive(6, s, pair_far, pair)
    for c in sent:
        c.wait_send()
    local.wait()


GROUP = 8


def scores_of(k_ref, q0, q1, s0_ref, s1_ref, times, write=None):
    def trip(i, carry):
        base = pl.multiple_of(i * GROUP, GROUP)
        rows0, rows1 = [], []
        for j in range(GROUP):
            raw = k_ref[base + j]
            kt = raw.astype(F32)
            rows0.append(jnp.sum(kt * q0, axis=0, keepdims=True))
            rows1.append(jnp.sum(kt * q1, axis=0, keepdims=True))
            if write is not None:
                write(base + j, raw)
        s0_ref[pl.ds(base, GROUP), :] = jnp.concatenate(rows0, axis=0)
        s1_ref[pl.ds(base, GROUP), :] = jnp.concatenate(rows1, axis=0)
        return carry
    lax.fori_loop(0, times // GROUP, trip, 0)


def mix_of(v_ref, w0_ref, w1_ref, times, init, write=None):
    def trip(i, carry):
        o0, o1 = carry
        base = pl.multiple_of(i * GROUP, GROUP)
        for j in range(GROUP):
            raw = v_ref[base + j]
            vt = raw.astype(F32)
            o0 = o0 + vt * w0_ref[pl.ds(base + j, 1), :]
            o1 = o1 + vt * w1_ref[pl.ds(base + j, 1), :]
            if write is not None:
                write(base + j, raw)
        return o0, o1
    return lax.fori_loop(0, times // GROUP, trip, init)


def soften(scores, mask):
    scores = jnp.where(mask, scores, -jnp.inf)
    weights = jnp.exp(scores - jnp.max(scores, axis=0, keepdims=True))
    return weights, jnp.sum(weights, axis=0, keepdims=True)


def self_kernel(*refs):
    for head in range(refs[1].shape[1]):
        self_head(head, *refs)


def self_head(head, pos_ref, q_ref, kn_ref, vn_ref, k_ref, v_ref, *rest):
    o_ref, ko_ref, vo_ref, s0_ref, s1_ref = rest[-5:]
    times, dim, lanes = k_ref.shape[1], k_ref.shape[3], k_ref.shape[4]
    kc, vc = k_ref.at[0, :, head], v_ref.at[0, :, head]
    pos = pos_ref[...]
    q = q_ref[0, head].astype(F32)
    kn = kn_ref[0, head]
    vn = vn_ref[0, head]
    q0, q1 = q[:, :lanes], q[:, lanes:]
    k0, k1 = kn[:, :lanes], kn[:, lanes:]
    v0, v1 = vn[:, :lanes], vn[:, lanes:]
    pack = 16
    here_b = jnp.broadcast_to(pos.astype(F32), (pack, lanes)).astype(BF16)
    after_b = jnp.broadcast_to((pos + 1).astype(F32), (pack, lanes)).astype(BF16)

    def writer(out_ref, new0, new1):
        def write(time, raw):
            step = jnp.broadcast_to(lax.convert_element_type(time, F32), (pack, lanes)).astype(BF16)
            first, second = here_b == step, after_b == step
            for r in range(0, dim, pack):
                rows = slice(r, r + pack)
                out_ref[0, time, head, rows] = jnp.where(first, new0[rows], jnp.where(second, new1[rows], raw[rows]))
        return write
    scores_of(kc, q0, q1, s0_ref, s1_ref, times, writer(ko_ref, k0, k1))
    s00 = jnp.sum(q0 * k0.astype(F32), axis=0, keepdims=True)
    s10 = jnp.sum(q1 * k0.astype(F32), axis=0, keepdims=True)
    s11 = jnp.sum(q1 * k1.astype(F32), axis=0, keepdims=True)
    t = lax.broadcasted_iota(jnp.int32, (times, lanes), 0)
    here, after = t == pos, t == pos + 1
    w0, sum0 = soften(jnp.where(here, s00, s0_ref[...]), t <= pos)
    w1, sum1 = soften(jnp.where(here, s10, jnp.where(after, s11, s1_ref[...])), t <= pos + 1)
    w0 = w0.astype(BF16).astype(F32)
    w1 = w1.astype(BF16).astype(F32)
    w00 = jnp.sum(jnp.where(here, w0, 0.0), axis=0, keepdims=True)
    w10 = jnp.sum(jnp.where(here, w1, 0.0), axis=0, keepdims=True)
    w11 = jnp.sum(jnp.where(after, w1, 0.0), axis=0, keepdims=True)
    s0_ref[...] = jnp.where(here, 0.0, w0)
    s1_ref[...] = jnp.where(here | after, 0.0, w1)
    o0, o1 = mix_of(vc, s0_ref, s1_ref, times,
                    (w00 * v0.astype(F32), w10 * v0.astype(F32) + w11 * v1.astype(F32)), writer(vo_ref, v0, v1))
    o_ref[head, :, :lanes] = (o0 / sum0).astype(BF16)
    o_ref[head, :, lanes:] = (o1 / sum1).astype(BF16)


def cross_kernel(*refs):
    for head in range(refs[1].shape[0]):
        cross_head(head, *refs)


def cross_head(head, len_ref, q_ref, k_ref, v_ref, o_ref, s0_ref, s1_ref):
    times, lanes = k_ref.shape[1], k_ref.shape[4]
    q = q_ref[head].astype(F32)
    scores_of(k_ref.at[0, :, head], q[:, :lanes], q[:, lanes:], s0_ref, s1_ref, times)
    mask = lax.broadcasted_iota(jnp.int32, (times, lanes), 0) < len_ref[...]
    w0, sum0 = soften(s0_ref[...], mask)
    w1, sum1 = soften(s1_ref[...], mask)
    s0_ref[...] = w0.astype(BF16).astype(F32)
    s1_ref[...] = w1.astype(BF16).astype(F32)
    zero = jnp.zeros((k_ref.shape[3], lanes), F32)
    o0, o1 = mix_of(v_ref.at[0, :, head], s0_ref, s1_ref, times, (zero, zero))
    o_ref[head, :, :lanes] = (o0 / sum0).astype(BF16)
    o_ref[head, :, lanes:] = (o1 / sum1).astype(BF16)


def turn(o_ref):
    return o_ref[...].astype(F32).T.astype(BF16)


def mid_kernel(layer, h_ref, o_ref, wide_ref, *rest):
    shards, (h_out, q_out, w, sems) = rest[:8], rest[8:]
    loads = [begin(load_slot(shards, 3 + j, w.at[j], sems.at[j])) for j in range(2)]
    o = turn(o_ref)
    finish(loads[0])
    h = h_ref[...] + (dot32(o, w[0]) + bias_row(wide_ref, layer, 3))
    h = norm_rows(h, *gain_row(wide_ref, layer, 0))
    h_out[...] = h
    finish(loads[1])
    q = (dot32(h.astype(BF16), w[1]) + bias_row(wide_ref, layer, 4)) * 0.125
    q_out[...] = q.T.astype(BF16)


def ffn_kernel(layer, h_ref, o_ref, wide_ref, *rest):
    shards, inner_shards, (h_out, hb_out, w, up, down, sems) = rest[:8], rest[8:16], rest[16:]
    part = shards[0].shape[1]
    width = h_ref.shape[1]
    blocks = up.shape[0]
    first = begin(load_slot(shards, 5, w, sems.at[0]))
    ups = [begin(load_slot(inner_shards, j, up.at[j], sems.at[1 + j])) for j in range(blocks)]
    downs = begin([pltpu.make_async_copy(ref.at[pl.ds(blocks, blocks)], down.at[own], sems.at[1 + blocks, i])
                   for i, (ref, own) in enumerate(zip(inner_shards, owners()))])
    o = turn(o_ref)
    finish(first)
    h = h_ref[...] + (dot32(o, w[...]) + bias_row(wide_ref, layer, 5))
    h = norm_rows(h, *gain_row(wide_ref, layer, 1))
    act = h.astype(BF16)
    acc = h + bias_row(wide_ref, layer, 12)
    per = width // (blocks * part)
    for j in range(blocks):
        finish(ups[j])
        u = dot32(act, up[j]) + bias_row(wide_ref, layer, 13 + j)
        g = (0.5 * u * (1.0 + lax.erf(u * ERF_SCALE))).astype(BF16)
        if j == 0:
            finish(downs)
        acc = acc + dot32(g, down[j * per:(j + 1) * per].reshape(width, width))
    h = norm_rows(acc, *gain_row(wide_ref, layer, 2))
    h_out[...] = h
    for i in range(hb_out.shape[0]):
        lanes = hb_out.shape[2]
        hb_out[i] = h[i * lanes:(i + 1) * lanes].T.astype(BF16)


def logits_kernel(hid_ref, tok_ref, bias_ref, out_ref, joined, bias):
    shards, _, _, lanes = hid_ref.shape
    tile = tok_ref.shape[0]
    step = pl.program_id(1)

    @pl.when(pl.program_id(0) == 0)
    def _():
        for i in range(shards):
            joined[step, :, i * lanes:(i + 1) * lanes] = hid_ref[i, step]

    @pl.when(step == 0)
    def _():
        for i in range(0, bias.shape[0], lanes):
            bias[i:i + lanes] = jnp.broadcast_to(bias_ref[0, :, i:i + lanes], (lanes, lanes)).T
    y = dot32(tok_ref[...], joined[step])
    for i in range(shards):
        cols = slice(i * lanes, (i + 1) * lanes)
        out_ref[0, :, cols] = y[:, cols] + bias[:tile]


def pack_kernel(up_ref, down_ref, out_ref):
    blocks, part, width = out_ref.shape[0] // 2, out_ref.shape[1], out_ref.shape[2]
    for j in range(blocks):
        out_ref[j] = up_ref[0, :, j * width:(j + 1) * width]
        out_ref[blocks + j] = down_ref[0, j * part:(j + 1) * part]


def params(limit_mib, sem='arbitrary'):
    return pltpu.CompilerParams(vmem_limit_bytes=limit_mib * MIB, dimension_semantics=(sem,))


def whole(shape):
    return pl.BlockSpec(shape, lambda i: (0,) * len(shape))


def run_small(*srcs):
    width = 8 * srcs[0].shape[-1]
    shapes = [(SLOTS,) + x.shape for x in srcs]
    return pl.pallas_call(
        small_kernel, name='small_gather',
        out_shape=(jax.ShapeDtypeStruct((40, width), F32), jax.ShapeDtypeStruct(shapes[5], jnp.int32)),
        in_specs=[pl.BlockSpec(memory_space=VM)] * 6, out_specs=[pl.BlockSpec(memory_space=VM)] * 2,
        scratch_shapes=[VM(shape, BF16) for shape in shapes[:5]] + [pltpu.SemaphoreType.DMA((6, 8)), pltpu.SemaphoreType.DMA((6, 8)), pltpu.SemaphoreType.DMA((6,))],
        compiler_params=pltpu.CompilerParams(collective_id=0, has_side_effects=True, vmem_limit_bytes=16 * MIB),
        cost_estimate=pl.CostEstimate(flops=4000000, bytes_accessed=1000000, **NONE),
    )(*srcs)


def run_embed(picked, ids, pos_rows, norm, vocab):
    _, rows, width = picked.shape
    block = VM((rows, width), BF16)
    return pl.pallas_call(
        functools.partial(embed_kernel, vocab), name='embed_sum',
        out_shape=jax.ShapeDtypeStruct((rows, width), F32),
        in_specs=[pl.BlockSpec(memory_space=VM)] * 4, out_specs=pl.BlockSpec(memory_space=VM),
        scratch_shapes=[VM((4, rows, width), BF16), VM((4, rows, width), BF16), VM((2, rows, width), BF16), block, block,
                        pltpu.SemaphoreType.DMA((9,)), pltpu.SemaphoreType.DMA((9,))],
        compiler_params=pltpu.CompilerParams(collective_id=1, has_side_effects=True, vmem_limit_bytes=32 * MIB),
        cost_estimate=pl.CostEstimate(flops=20000000, bytes_accessed=picked.size * 4, **NONE),
    )(picked, ids, pos_rows, norm)


def run_gather(rows):
    return pl.pallas_call(
        gather_kernel, name='row_gather',
        out_shape=jax.ShapeDtypeStruct((8,) + rows.shape, rows.dtype),
        in_specs=[pl.BlockSpec(memory_space=VM)], out_specs=pl.BlockSpec(memory_space=VM),
        scratch_shapes=[pltpu.SemaphoreType.DMA((7, rows.shape[0])), pltpu.SemaphoreType.DMA((7, rows.shape[0])), pltpu.SemaphoreType.DMA],
        compiler_params=pltpu.CompilerParams(collective_id=2, has_side_effects=True, vmem_limit_bytes=32 * MIB),
        cost_estimate=pl.CostEstimate(flops=20000000, bytes_accessed=rows.size * 18, **NONE),
    )(rows)


def run_qkv(layer, x, shards, wide):
    rows, width = x.shape
    return pl.pallas_call(
        functools.partial(qkv_kernel, layer), grid=(1,), name='qkv',
        out_shape=jax.ShapeDtypeStruct((3, width, rows), BF16),
        in_specs=[whole((rows, width)), whole(wide.shape)] + [HBM] * 8,
        out_specs=whole((3, width, rows)),
        scratch_shapes=[VM((3, width, width), BF16), pltpu.SemaphoreType.DMA((3, 8))],
        compiler_params=params(53),
        cost_estimate=pl.CostEstimate(flops=2 * rows * width * width * 3, bytes_accessed=6 * width * width, **NONE),
    )(x, wide, *shards)


def run_self(layer, pos, qkv, cache_k, cache_v, new_k, new_v, per=2):
    _, times, heads, dim, lanes = cache_k.shape
    rows = qkv.shape[-1]
    qkv = qkv.reshape(3, heads, dim, rows)
    cache_spec = pl.BlockSpec((1, times, per, dim, lanes), lambda h: (layer, 0, h, 0, 0))
    args = [pos, qkv, qkv, qkv, cache_k, cache_v]
    specs = [whole((1, lanes))] + [pl.BlockSpec((1, per, dim, rows), functools.partial(lambda j, h: (j, h, 0, 0), j)) for j in range(3)]
    specs += [cache_spec, cache_spec]
    aliases = {}
    if new_k is not None:
        args += [new_k, new_v]
        specs += [pl.BlockSpec(memory_space=pl.ANY)] * 2
        aliases = {6: 1, 7: 2}
    return pl.pallas_call(
        self_kernel, grid=(heads // per,), name='self_attn',
        out_shape=(jax.ShapeDtypeStruct((heads, dim, rows), BF16),
                   jax.ShapeDtypeStruct(cache_k.shape, BF16), jax.ShapeDtypeStruct(cache_v.shape, BF16)),
        in_specs=specs,
        out_specs=(pl.BlockSpec((per, dim, rows), lambda h: (h, 0, 0)), cache_spec, cache_spec),
        scratch_shapes=[VM((times, lanes), F32), VM((times, lanes), F32)],
        input_output_aliases=aliases,
        compiler_params=params(53),
        cost_estimate=pl.CostEstimate(flops=8 * heads * dim * rows * times, bytes_accessed=8 * times * heads * dim * lanes, **NONE),
    )(*args)


def run_cross(layer, lens, q, cross_k, cross_v, per=3):
    _, times, heads, dim, lanes = cross_k.shape
    rows = q.shape[-1]
    q = q.reshape(heads, dim, rows)
    spec = pl.BlockSpec((1, times, per, dim, lanes), lambda h: (layer, 0, h, 0, 0))
    row_spec = pl.BlockSpec((per, dim, rows), lambda h: (h, 0, 0))
    return pl.pallas_call(
        cross_kernel, grid=(heads // per,), name='cross_attn',
        out_shape=jax.ShapeDtypeStruct((heads, dim, rows), BF16),
        in_specs=[whole((1, lanes)), row_spec, spec, spec],
        out_specs=row_spec,
        scratch_shapes=[VM((times, lanes), F32), VM((times, lanes), F32)],
        compiler_params=params(53),
        cost_estimate=pl.CostEstimate(flops=8 * heads * dim * rows * times, bytes_accessed=4 * times * heads * dim * lanes, **NONE),
    )(lens, q, cross_k, cross_v)


def run_mid(layer, h, o, shards, wide):
    rows, width = h.shape
    return pl.pallas_call(
        functools.partial(mid_kernel, layer), grid=(1,), name='mid',
        out_shape=(jax.ShapeDtypeStruct((rows, width), F32), jax.ShapeDtypeStruct((width, rows), BF16)),
        in_specs=[whole((rows, width)), whole((width, rows)), whole(wide.shape)] + [HBM] * 8,
        out_specs=(whole((rows, width)), whole((width, rows))),
        scratch_shapes=[VM((2, width, width), BF16), pltpu.SemaphoreType.DMA((2, 8))],
        compiler_params=params(53),
        cost_estimate=pl.CostEstimate(flops=4 * rows * width * width, bytes_accessed=4 * width * width, **NONE),
    )(h, o.reshape(width, rows), wide, *shards)


def run_ffn(layer, h, o, shards, inner_shards, wide):
    rows, width = h.shape
    part = shards[0].shape[1]
    blocks = inner_shards[0].shape[0] // 2
    inner = blocks * width
    return pl.pallas_call(
        functools.partial(ffn_kernel, layer), grid=(1,), name='ffn',
        out_shape=(jax.ShapeDtypeStruct((rows, width), F32), jax.ShapeDtypeStruct((2, width, rows // 2), BF16)),
        in_specs=[whole((rows, width)), whole((width, rows)), whole(wide.shape)] + [HBM] * 16,
        out_specs=(whole((rows, width)), whole((2, width, rows // 2))),
        scratch_shapes=[VM((width, width), BF16), VM((blocks, width, width), BF16), VM((8, blocks, part, width), BF16),
                        pltpu.SemaphoreType.DMA((blocks + 2, 8))],
        compiler_params=params(53),
        cost_estimate=pl.CostEstimate(flops=4 * rows * width * inner, bytes_accessed=4 * width * inner, **NONE),
    )(h, o.reshape(width, rows), wide, *shards, *inner_shards)


def run_pack(layer, up, down):
    _, part, inner = up.shape
    width = down.shape[2]
    return pl.pallas_call(
        pack_kernel, grid=(1,), name='pack',
        out_shape=jax.ShapeDtypeStruct((2 * inner // width, part, width), BF16),
        in_specs=[pl.BlockSpec((1, part, inner), lambda i: (layer, 0, 0)), pl.BlockSpec((1,) + down.shape[1:], lambda i: (layer, 0, 0))],
        out_specs=whole((2 * inner // width, part, width)),
        compiler_params=params(16),
        cost_estimate=pl.CostEstimate(flops=2000000, bytes_accessed=8 * part * inner, **NONE),
    )(up, down)


def run_logits(hid, tok, bias, tile=1568):
    shards, steps, width, lanes = hid.shape
    vocab = tok.shape[0]
    rows = shards * lanes
    tiles = pl.cdiv(vocab, tile)
    bias = jnp.pad(bias, (0, tiles * tile - vocab)).reshape(tiles, 1, tile)
    bias = jnp.pad(bias, ((0, 0), (0, 0), (0, -tile % lanes)))
    return pl.pallas_call(
        logits_kernel, grid=(tiles, steps), name='logits',
        out_shape=jax.ShapeDtypeStruct((steps, vocab, rows), F32),
        in_specs=[pl.BlockSpec(hid.shape, lambda v, s: (0, 0, 0, 0)),
                  pl.BlockSpec((tile, width), lambda v, s: (v, 0)),
                  pl.BlockSpec((1, 1, bias.shape[2]), lambda v, s: (v, 0, 0))],
        out_specs=pl.BlockSpec((1, tile, rows), lambda v, s: (s, v, 0)),
        scratch_shapes=[VM((steps, width, rows), BF16), VM((bias.shape[2], lanes), F32)],
        compiler_params=pltpu.CompilerParams(vmem_limit_bytes=56 * MIB, dimension_semantics=('arbitrary', 'arbitrary')),
        cost_estimate=pl.CostEstimate(flops=2 * steps * rows * vocab * width, bytes_accessed=4 * steps * rows * vocab, **NONE),
    )(hid, tok, bias)


def solution(mesh):
    cache_spec = P(None, 'fsdp')
    in_specs = (P('fsdp'), P('fsdp'), P('fsdp'), cache_spec, cache_spec, cache_spec, cache_spec,
                P(None, None, 'fsdp'), P(None, None, 'fsdp'), P(None, 'fsdp'), P(None, 'fsdp'),
                P(None, 'fsdp'), P(None, 'fsdp'), P(None, None, 'fsdp'), P(None, None, 'fsdp'),
                P('fsdp'), P(), P(), P('fsdp'))
    out_specs = (P(None, None, 'fsdp'), cache_spec, cache_spec)


    def decode(tokens, positions, src_len, self_k, self_v, cross_k, cross_v, attn_w, attn_b, fc1_w, fc1_b, fc2_w, fc2_b, ln_gain, ln_bias, tok_embed, pos_embed, emb_norm, logit_bias):
        me = lax.axis_index('fsdp')
        shards = lax.axis_size('fsdp')
        layers = attn_w.shape[0]
        _, steps = tokens.shape
        width = attn_w.shape[3]
        vocab = tok_embed.shape[0]

        flip = lambda z: z.transpose(1, 0, 2)
        wide, ids = run_small(flip(attn_b), flip(ln_gain), flip(ln_bias), fc2_b, fc1_b, tokens.T)
        local_ids = jnp.clip(ids[:shards].reshape(-1) - me * vocab, 0, vocab - 1)
        picked = tok_embed.at[local_ids].get(mode='promise_in_bounds').reshape(shards, -1, width)
        row_pos = jnp.concatenate([positions + 2 + s for s in range(steps)])
        pos_rows = pos_embed.at[row_pos].get(mode='promise_in_bounds')
        hidden = run_embed(picked, ids, pos_rows, emb_norm, vocab)

        to_lanes = (0, 2, 3, 4, 1)
        old_k, old_v, ck, cv = [c.transpose(to_lanes) for c in (self_k, self_v, cross_k, cross_v)]
        pos = positions[None, :]
        lens = src_len[None, :]
        new_k = new_v = None
        after = [wide, hidden]
        attn = [attn_w[layer] for layer in range(layers)]
        inner = [run_pack(layer, fc1_w, fc2_w) for layer in range(layers)]
        attn[0], _ = lax.optimization_barrier((attn[0], after[0]))
        inner[0], _ = lax.optimization_barrier((inner[0], after[1]))
        attn_shards = [spread(attn[layer]) for layer in range(layers)]
        inner_shards = [spread(inner[layer]) for layer in range(layers)]
        for layer in range(layers):
            w = attn_shards[layer]
            qkv = run_qkv(layer, hidden, w, wide)
            o, new_k, new_v = run_self(layer, pos, qkv, old_k, old_v, new_k, new_v)
            hidden, q = run_mid(layer, hidden, o, w, wide)
            o = run_cross(layer, lens, q, ck, cv)
            hidden, hidden_b = run_ffn(layer, hidden, o, w, inner_shards[layer], wide)
        rows = run_gather(hidden_b)
        logits = run_logits(rows, tok_embed, logit_bias)
        back = (0, 4, 1, 2, 3)
        return logits.transpose(0, 2, 1), new_k.transpose(back), new_v.transpose(back)

    return jax.shard_map(decode, mesh=mesh, in_specs=in_specs, out_specs=out_specs, check_vma=False)
```

time: 552 us -> 330 us (0.60); the launches traced: 545 us -> 329 us
  other arithmetic: 243 us -> 0.04 us
  Pallas kernels: 0 us -> 191 us
  blocking collectives: 141 us -> 0 us
  matrix products: 102 us -> 0 us
  waiting for transfers between devices: 2 us -> 89.8 us
  starting transfers between devices: 0.36 us -> 17.2 us
  between operations: 16.1 us -> 1.18 us
  local copies, waits for them, and re-layouts: 40.9 us -> 29.4 us
    pallas_call x0 -> x16, Pallas kernels: none -> 191 us  [the longest x2 47.2 us: run_self(): pl.pallas_call(self_kernel, grid=(heads // per,), name='self_attn', out_s...]
    all_gather x9 -> x0, blocking collectives: 118 us -> none  [the longest x2 28.8 us: local_decode(): ln_gains = lax.all_gather(ln_gain[layer_idx], 'fsdp', axis=1, tiled=True)]
    dot_general x22 -> x0, matrix products: 102 us -> none  [the longest x16 51.4 us: project(): jnp.dot(act_rows, weight, preferred_element_type=jnp.float32)]
    ppermute x0 -> x28, waiting for transfers between devices: none -> 89.8 us  [hop(): return lax.ppermute(block, 'fsdp', pairs)]
    another operation x3 -> x0, other arithmetic: 69.2 us -> none  [local_decode(): return (jnp.stack(step_logits), jnp.stack(cache_k), jnp.stack(cache_v))]
    unnamed x15 -> x0, other arithmetic: 39.4 us -> none
    select_n x2, other arithmetic: 36.3 us -> 0.02 us  [the longest x1 0.01 us: decode(): tok_embed.at[local_ids].get(mode='promise_in_bounds')]
    add x5 -> x0, other arithmetic: 35.4 us -> none  [the longest x2 19.2 us: project(): jnp.dot(act_rows, weight, preferred_element_type=jnp.float32)]
  transfers between devices with their start and end apart: 9 -> 28, of which waited for: 0 -> 7; matrix products, arithmetic and copies ran while one was open for 52% -> 5% of each run, Pallas kernels for 0% -> 38%
where the time goes in v1:
time: 330 us; the launch traced here: 329 us
  Pallas kernels  191 us (58%)
  waiting for transfers between devices  89.8 us (27%)
  local copies, waits for them, and re-layouts  29.4 us (9%)
  starting transfers between devices  17.2 us (5%)
    ppermute x28, waiting for transfers between devices, hop(): return lax.ppermute(block, 'fsdp', pairs)  89.8 us
    pallas_call x2, Pallas kernels, run_self(): pl.pallas_call(self_kernel, grid=(heads // per,), name='self_attn', out_s...  47.2 us
    pallas_call x1, Pallas kernels, run_logits(): pl.pallas_call(logits_kernel, grid=(tiles, steps), name='logits', out_sha...  31.2 us
    pallas_call x1, Pallas kernels, run_embed(): pl.pallas_call(functools.partial(embed_kernel, vocab), name='embed_sum',...  31.2 us
    pallas_call x2, Pallas kernels, run_ffn(): pl.pallas_call(functools.partial(ffn_kernel, layer), grid=(1,), name='ffn...  19.9 us
    pallas_call x1, Pallas kernels, run_gather(): pl.pallas_call(gather_kernel, name='row_gather', out_shape=jax.ShapeDtype...  18.7 us
    pallas_call x2, Pallas kernels, run_cross(): pl.pallas_call(cross_kernel, grid=(heads // per,), name='cross_attn', out...  17.3 us
    ppermute x28, starting transfers between devices, hop(): return lax.ppermute(block, 'fsdp', pairs)  17.2 us
  transfers between devices with their start and end apart: 28, of which 7 were waited for; matrix products, arithmetic and copies ran while one was open for 5% of the time, Pallas kernels for 38%

profile of v1, /device:TPU:0, one launch (start us, length us, event | category | flops | bytes accessed | tf_op | source)
XLA Modules:
  0.0 328.9 jit_solution(6025115842423944557)
XLA Ops:
  0.7 2.6 slice_bitcast_fusion
  3.3 8.0 %small_gather.1 = (f32[40,768]{1,0:T(8,128)S(1)}, s32[16,2,128]{2,1,0:T(2,128)S(1)}) custom-call(bf16[6,2,96]{2,1,0:T(2,128)(2,1)S(1)} %bitcast.44, bf16[3,2,96]{2,1,0:T(2,128)(2,1)S(1)} %bitcast.45, bf16[3,2,96]{2,1,0:T(2,128)(2,1)S(1)} %bitcast.46, bf16[2,96]{1,0:T(2,128)(2,1)S(1)} %copy-done.21, bf16[2,384]{1,0:T(2,128)(2,1)S(1)} %copy-done.19, ...), custom_call_target="tpu_custom_call" | custom-call | flops 4000000 | bytes 1000000 | tf_op jit(solution)/shard_map/small_gather/pallas_call | solution.py:441
  15.5 15.0 %gather_fusion = bf16[2048,768]{1,0:T(8,128)(2,1)} fusion(bf16[6256,768]{1,0:T(8,128)(2,1)} %tok_ref.1, s32[2048]{0:T(1024)S(1)} %broadcast_clamp_fusion), kind=kCustom, calls=%fused_computation | custom fusion | bytes 6299648 | tf_op jit(solution)/shard_map/gather | solution.py:615
  30.5 1.9 gather_fusion.1
  35.1 2.2 copy-done.2
  37.4 31.2 %embed_sum.1.x_ref.h_ref = f32[256,768]{1,0:T(8,128)S(1)} custom-call(bf16[8,256,768]{2,1,0:T(8,128)(2,1)S(1)} %bitcast.33, s32[16,2,128]{2,1,0:T(2,128)S(1)} %get-tuple-element.19.ids, bf16[256,768]{1,0:T(8,128)(2,1)S(1)} %copy-done.12, bf16[2,768]{1,0:T(2,128)(2,1)S(1)} %copy-done.13), custom_call_target="tpu_custom_call" | custom-call | flops 20000000 | bytes 6291456 | tf_op jit(solution)/shard_map/embed_sum/pallas_call | solution.py:454
  72.9 24.2 %collective-permute-done.7.rest_9_ = bf16[8,96,768]{2,1,0:T(8,128)(2,1)S(1)} collective-permute-done((bf16[8,96,768]{2,1,0:T(8,128)(2,1)S(1)}, bf16[8,96,768]{2,1,0:T(8,128)(2,1)S(1)}, u32[]{:S(2)}, u32[]{:S(2)}) %collective-permute-start.7) | collective-permute-done | bytes 1179680 | tf_op jit(solution)/shard_map/ppermute | solution.py:63
  100.2 22.3 %collective-permute-done.21.rest_9_ = bf16[8,96,768]{2,1,0:T(8,128)(2,1)} collective-permute-done((bf16[8,96,768]{2,1,0:T(8,128)(2,1)S(1)}, bf16[8,96,768]{2,1,0:T(8,128)(2,1)}, u32[]{:S(2)}, u32[]{:S(2)}) %collective-permute-start.21) | collective-permute-done | bytes 1179680 | tf_op jit(solution)/shard_map/ppermute | solution.py:63
  124.0 7.7 %collective-permute-done.2.rest_3_ = bf16[6,96,768]{2,1,0:T(8,128)(2,1)S(1)} collective-permute-done((bf16[6,96,768]{2,1,0:T(8,128)(2,1)}, bf16[6,96,768]{2,1,0:T(8,128)(2,1)S(1)}, u32[]{:S(2)}, u32[]{:S(2)}) %collective-permute-start.2) | collective-permute-done | bytes 884768 | tf_op jit(solution)/shard_map/ppermute | solution.py:63
  132.9 21.0 %collective-permute-done.16.rest_3_ = bf16[6,96,768]{2,1,0:T(8,128)(2,1)S(1)} collective-permute-done((bf16[6,96,768]{2,1,0:T(8,128)(2,1)}, bf16[6,96,768]{2,1,0:T(8,128)(2,1)S(1)}, u32[]{:S(2)}, u32[]{:S(2)}) %collective-permute-start.16) | collective-permute-done | bytes 884768 | tf_op jit(solution)/shard_map/ppermute | solution.py:63
  157.1 13.7 %collective-permute-done.23.rest_11_ = bf16[8,96,768]{2,1,0:T(8,128)(2,1)} collective-permute-done((bf16[8,96,768]{2,1,0:T(8,128)(2,1)}, bf16[8,96,768]{2,1,0:T(8,128)(2,1)}, u32[]{:S(2)}, u32[]{:S(2)}) %collective-permute-start.23) | collective-permute-done | bytes 1179680 | tf_op jit(solution)/shard_map/ppermute | solution.py:63
  174.0 4.4 %qkv.2 = bf16[3,768,256]{2,1,0:T(8,128)(2,1)} custom-call(f32[256,768]{1,0:T(8,128)S(1)} %embed_sum.1.x_ref.h_ref, f32[40,768]{1,0:T(8,128)S(1)} %get-tuple-element.20.wide_ref, bf16[6,96,768]{2,1,0:T(8,128)(2,1)} %get-tuple-element.21.rest_0_, bf16[6,96,768]{2,1,0:T(8,128)(2,1)} %collective-permute-done.rest_1_, ...), custom_call_target="tpu_custom_call" | custom-call | flops 905969664 | bytes 3538944 | tf_op jit(solution)/shard_map/qkv/pallas_call | solution.py:478
  178.5 23.6 %self_attn.2 = (bf16[12,64,256]{2,1,0:T(8,128)(2,1)S(1)}, bf16[2,64,12,64,128]{4,3,2,1,0:T(8,128)(2,1)}, bf16[2,64,12,64,128]{4,3,2,1,0:T(8,128)(2,1)}) custom-call(s32[1,128]{1,0:T(1,128)S(1)} %bitcast.42, bf16[3,12,64,256]{3,2,1,0:T(8,128)(2,1)} %bitcast.58, bf16[3,12,64,256]{3,2,1,0:T(8,128)(2,1)} %bitcast.59, bf16[3,12,64,256]{3,2,1,0:T(8,128)(2,1)} %bitcast.60, ...), custom_call_target="tpu_custom_call" | custom-call | flops 100663296 | bytes 50331648 | tf_op jit(solution)/shard_map/self_attn/pallas_call | solution.py:502
  202.1 4.4 %mid.2 = (f32[256,768]{1,0:T(8,128)}, bf16[768,256]{1,0:T(8,128)(2,1)S(1)}) custom-call(f32[256,768]{1,0:T(8,128)} %copy-done.3, bf16[768,256]{1,0:T(8,128)(2,1)S(1)} %bitcast.37, f32[40,768]{1,0:T(8,128)S(1)} %get-tuple-element.20.wide_ref, bf16[6,96,768]{2,1,0:T(8,128)(2,1)} %get-tuple-element.21.rest_0_, ...), custom_call_target="tpu_custom_call" | custom-call | flops 603979776 | bytes 2359296 | tf_op jit(solution)/shard_map/mid/pallas_call | solution.py:534
  206.5 8.8 %cross_attn.2 = bf16[12,64,256]{2,1,0:T(8,128)(2,1)S(1)} custom-call(s32[1,128]{1,0:T(1,128)S(1)} %bitcast.40, bf16[12,64,256]{2,1,0:T(8,128)(2,1)S(1)} %bitcast.38, bf16[2,32,12,64,128]{4,3,2,1,0:T(8,128)(2,1)} %bitcast.52, bf16[2,32,12,64,128]{4,3,2,1,0:T(8,128)(2,1)} %bitcast.54), custom_call_target="tpu_custom_call" | custom-call | flops 50331648 | bytes 12582912 | tf_op jit(solution)/shard_map/cross_attn/pallas_call | solution.py:521
  215.3 10.0 %ffn.2 = (f32[256,768]{1,0:T(8,128)}, bf16[2,768,128]{2,1,0:T(8,128)(2,1)}) custom-call(f32[256,768]{1,0:T(8,128)} %get-tuple-element.23.h_ref, bf16[768,256]{1,0:T(8,128)(2,1)S(1)} %bitcast.35, f32[40,768]{1,0:T(8,128)S(1)} %get-tuple-element.20.wide_ref, bf16[6,96,768]{2,1,0:T(8,128)(2,1)} %get-tuple-element.21.rest_0_, ...), custom_call_target="tpu_custom_call" | custom-call | flops 2415919104 | bytes 9437184 | tf_op jit(solution)/shard_map/ffn/pallas_call | solution.py:550
  226.4 4.4 %qkv.3 = bf16[3,768,256]{2,1,0:T(8,128)(2,1)} custom-call(f32[256,768]{1,0:T(8,128)S(1)} %copy-done.11, f32[40,768]{1,0:T(8,128)S(1)} %get-tuple-element.20.wide_ref, bf16[6,96,768]{2,1,0:T(8,128)(2,1)} %copy-done.22, bf16[6,96,768]{2,1,0:T(8,128)(2,1)} %collective-permute-done.14.rest_1_, bf16[6,96,768]{2,1,0:T(8,128)(2,1)} %collective-permute-done.15.rest_2_, ...), custom_call_target="tpu_custom_call" | custom-call | flops 905969664 | bytes 3538944 | tf_op jit(solution)/shard_map/qkv/pallas_call | solution.py:478
  230.9 23.6 %self_attn.3 = (bf16[12,64,256]{2,1,0:T(8,128)(2,1)S(1)}, bf16[2,64,12,64,128]{4,3,2,1,0:T(8,128)(2,1)}, bf16[2,64,12,64,128]{4,3,2,1,0:T(8,128)(2,1)}) custom-call(s32[1,128]{1,0:T(1,128)S(1)} %bitcast.43, bf16[3,12,64,256]{3,2,1,0:T(8,128)(2,1)} %bitcast.61, bf16[3,12,64,256]{3,2,1,0:T(8,128)(2,1)} %bitcast.62, ...), custom_call_target="tpu_custom_call", output_to_operand_aliasing={{1}: (6, {}), {2}: (7, {})} | custom-call | flops 100663296 | bytes 50331648 | tf_op jit(solution)/shard_map/self_attn/pallas_call | solution.py:502
  254.5 4.3 %mid.3 = (f32[256,768]{1,0:T(8,128)}, bf16[768,256]{1,0:T(8,128)(2,1)S(1)}) custom-call(f32[256,768]{1,0:T(8,128)} %get-tuple-element.26.x_ref.h_ref, bf16[768,256]{1,0:T(8,128)(2,1)S(1)} %bitcast.36, f32[40,768]{1,0:T(8,128)S(1)} %get-tuple-element.20.wide_ref, bf16[6,96,768]{2,1,0:T(8,128)(2,1)} %copy-done.22, ...), custom_call_target="tpu_custom_call" | custom-call | flops 603979776 | bytes 2359296 | tf_op jit(solution)/shard_map/mid/pallas_call | solution.py:534
  258.8 8.6 %cross_attn.3 = bf16[12,64,256]{2,1,0:T(8,128)(2,1)S(1)} custom-call(s32[1,128]{1,0:T(1,128)S(1)} %bitcast.41, bf16[12,64,256]{2,1,0:T(8,128)(2,1)S(1)} %bitcast.39, bf16[2,32,12,64,128]{4,3,2,1,0:T(8,128)(2,1)} %bitcast.53, bf16[2,32,12,64,128]{4,3,2,1,0:T(8,128)(2,1)} %bitcast.55), custom_call_target="tpu_custom_call" | custom-call | flops 50331648 | bytes 12582912 | tf_op jit(solution)/shard_map/cross_attn/pallas_call | solution.py:521
  267.5 9.9 %ffn.3 = (f32[256,768]{1,0:T(8,128)}, bf16[2,768,128]{2,1,0:T(8,128)(2,1)S(1)}) custom-call(f32[256,768]{1,0:T(8,128)} %get-tuple-element.30.h_ref, bf16[768,256]{1,0:T(8,128)(2,1)S(1)} %bitcast.34, f32[40,768]{1,0:T(8,128)S(1)} %get-tuple-element.20.wide_ref, bf16[6,96,768]{2,1,0:T(8,128)(2,1)} %copy-done.22, ...), custom_call_target="tpu_custom_call" | custom-call | flops 2415919104 | bytes 9437184 | tf_op jit(solution)/shard_map/ffn/pallas_call | solution.py:550
  277.4 18.7 %row_gather.1.hid_ref = bf16[8,2,768,128]{3,2,1,0:T(8,128)(2,1)S(1)} custom-call(bf16[2,768,128]{2,1,0:T(8,128)(2,1)S(1)} %get-tuple-element.32.src), custom_call_target="tpu_custom_call" | custom-call | flops 20000000 | bytes 3538944 | tf_op jit(solution)/shard_map/row_gather/pallas_call | solution.py:466
  296.0 1.6 copy-done.10
  297.7 31.2 %logits.1 = f32[2,6256,1024]{2,1,0:T(8,128)} custom-call(bf16[8,2,768,128]{3,2,1,0:T(8,128)(2,1)} %copy-done.10, bf16[6256,768]{1,0:T(8,128)(2,1)} %tok_ref.1, f32[4,1,1664]{2,1,0:T(1,128)} %pad.9.bias_ref), custom_call_target="tpu_custom_call" | custom-call | flops 19679674368 | bytes 51249152 | tf_op jit(solution)/shard_map/logits/pallas_call | solution.py:582
  (136 shorter events, 24.4 us)
Async XLA Ops:
  11.3 57.3 %collective-permute-start = (bf16[6,96,768]{2,1,0:T(8,128)(2,1)}, bf16[6,96,768]{2,1,0:T(8,128)(2,1)}, u32[]{:S(2)}, u32[]{:S(2)}) collective-permute-start(bf16[6,96,768]{2,1,0:T(8,128)(2,1)} %get-tuple-element.21.rest_0_), channel_id=1, source_target_pairs={{0,2},{1,5},{2,0},{3,7},{4,6},{5,1},{6,4},{7,3}} | collective-permute-start | bytes 2654216 | tf_op jit(solution)/shard_map/ppermute | solution.py:63
  12.8 55.8 %collective-permute-start.1 = (bf16[6,96,768]{2,1,0:T(8,128)(2,1)}, bf16[6,96,768]{2,1,0:T(8,128)(2,1)}, u32[]{:S(2)}, u32[]{:S(2)}) collective-permute-start(bf16[6,96,768]{2,1,0:T(8,128)(2,1)} %get-tuple-element.21.rest_0_), channel_id=1, source_target_pairs={{0,4},{1,3},{2,6},{3,1},{4,0},{5,7},{6,2},{7,5}} | collective-permute-start | bytes 2654216 | tf_op jit(solution)/shard_map/ppermute | solution.py:63
  14.2 55.9 %collective-permute-start.3 = (bf16[6,96,768]{2,1,0:T(8,128)(2,1)}, bf16[6,96,768]{2,1,0:T(8,128)(2,1)}, u32[]{:S(2)}, u32[]{:S(2)}) collective-permute-start(bf16[6,96,768]{2,1,0:T(8,128)(2,1)} %get-tuple-element.21.rest_0_), channel_id=1, source_target_pairs={{0,1},{1,0},{2,3},{3,2},{4,5},{5,4},{6,7},{7,6}} | collective-permute-start | bytes 2654216 | tf_op jit(solution)/shard_map/ppermute | solution.py:63
  14.2 57.1 %collective-permute-start.14 = (bf16[6,96,768]{2,1,0:T(8,128)(2,1)S(1)}, bf16[6,96,768]{2,1,0:T(8,128)(2,1)}, u32[]{:S(2)}, u32[]{:S(2)}) collective-permute-start(bf16[6,96,768]{2,1,0:T(8,128)(2,1)S(1)} %get-tuple-element.35.rest_0_), channel_id=1, source_target_pairs={{0,2},{1,5},{2,0},{3,7},{4,6},{5,1},{6,4},{7,3}} | collective-permute-start | bytes 2654216 | tf_op jit(solution)/shard_map/ppermute | solution.py:63
  14.8 56.6 %collective-permute-start.15 = (bf16[6,96,768]{2,1,0:T(8,128)(2,1)S(1)}, bf16[6,96,768]{2,1,0:T(8,128)(2,1)}, u32[]{:S(2)}, u32[]{:S(2)}) collective-permute-start(bf16[6,96,768]{2,1,0:T(8,128)(2,1)S(1)} %get-tuple-element.35.rest_0_), channel_id=1, source_target_pairs={{0,4},{1,3},{2,6},{3,1},{4,0},{5,7},{6,2},{7,5}} | collective-permute-start | bytes 2654216 | tf_op jit(solution)/shard_map/ppermute | solution.py:63
  68.6 28.4 %collective-permute-start.7 = (bf16[8,96,768]{2,1,0:T(8,128)(2,1)S(1)}, bf16[8,96,768]{2,1,0:T(8,128)(2,1)S(1)}, u32[]{:S(2)}, u32[]{:S(2)}) collective-permute-start(bf16[8,96,768]{2,1,0:T(8,128)(2,1)S(1)} %pack.2.rest_8_), channel_id=1, source_target_pairs={{0,2},{1,5},{2,0},{3,7},{4,6},{5,1},{6,4},{7,3}} | collective-permute-start | bytes 3538952 | tf_op jit(solution)/shard_map/ppermute | solution.py:63
  70.2 28.8 %collective-permute-start.8 = (bf16[8,96,768]{2,1,0:T(8,128)(2,1)S(1)}, bf16[8,96,768]{2,1,0:T(8,128)(2,1)S(1)}, u32[]{:S(2)}, u32[]{:S(2)}) collective-permute-start(bf16[8,96,768]{2,1,0:T(8,128)(2,1)S(1)} %pack.2.rest_8_), channel_id=1, source_target_pairs={{0,4},{1,3},{2,6},{3,1},{4,0},{5,7},{6,2},{7,5}} | collective-permute-start | bytes 3538952 | tf_op jit(solution)/shard_map/ppermute | solution.py:63
  71.3 27.7 %collective-permute-start.10 = (bf16[8,96,768]{2,1,0:T(8,128)(2,1)S(1)}, bf16[8,96,768]{2,1,0:T(8,128)(2,1)S(1)}, u32[]{:S(2)}, u32[]{:S(2)}) collective-permute-start(bf16[8,96,768]{2,1,0:T(8,128)(2,1)S(1)} %pack.2.rest_8_), channel_id=1, source_target_pairs={{0,1},{1,0},{2,3},{3,2},{4,5},{5,4},{6,7},{7,6}} | collective-permute-start | bytes 3538952 | tf_op jit(solution)/shard_map/ppermute | solution.py:63
  71.5 51.0 %collective-permute-start.21 = (bf16[8,96,768]{2,1,0:T(8,128)(2,1)S(1)}, bf16[8,96,768]{2,1,0:T(8,128)(2,1)}, u32[]{:S(2)}, u32[]{:S(2)}) collective-permute-start(bf16[8,96,768]{2,1,0:T(8,128)(2,1)S(1)} %pack.3.rest_8_), channel_id=1, source_target_pairs={{0,2},{1,5},{2,0},{3,7},{4,6},{5,1},{6,4},{7,3}} | collective-permute-start | bytes 3538952 | tf_op jit(solution)/shard_map/ppermute | solution.py:63
  72.1 50.4 %collective-permute-start.22 = (bf16[8,96,768]{2,1,0:T(8,128)(2,1)S(1)}, bf16[8,96,768]{2,1,0:T(8,128)(2,1)}, u32[]{:S(2)}, u32[]{:S(2)}) collective-permute-start(bf16[8,96,768]{2,1,0:T(8,128)(2,1)S(1)} %pack.3.rest_8_), channel_id=1, source_target_pairs={{0,4},{1,3},{2,6},{3,1},{4,0},{5,7},{6,2},{7,5}} | collective-permute-start | bytes 3538952 | tf_op jit(solution)/shard_map/ppermute | solution.py:63
  97.1 34.7 %collective-permute-start.2 = (bf16[6,96,768]{2,1,0:T(8,128)(2,1)}, bf16[6,96,768]{2,1,0:T(8,128)(2,1)S(1)}, u32[]{:S(2)}, u32[]{:S(2)}) collective-permute-start(bf16[6,96,768]{2,1,0:T(8,128)(2,1)} %collective-permute-done.rest_1_), channel_id=1, source_target_pairs={{0,4},{1,3},{2,6},{3,1},{4,0},{5,7},{6,2},{7,5}} | collective-permute-start | bytes 2654216 | tf_op jit(solution)/shard_map/ppermute | solution.py:63
  99.0 33.4 %collective-permute-start.4 = (bf16[6,96,768]{2,1,0:T(8,128)(2,1)}, bf16[6,96,768]{2,1,0:T(8,128)(2,1)}, u32[]{:S(2)}, u32[]{:S(2)}) collective-permute-start(bf16[6,96,768]{2,1,0:T(8,128)(2,1)} %collective-permute-done.rest_1_), channel_id=1, source_target_pairs={{0,1},{1,0},{2,3},{3,2},{4,5},{5,4},{6,7},{7,6}} | collective-permute-start | bytes 2654216 | tf_op jit(solution)/shard_map/ppermute | solution.py:63
  99.0 56.4 %collective-permute-start.9 = (bf16[8,96,768]{2,1,0:T(8,128)(2,1)S(1)}, bf16[8,96,768]{2,1,0:T(8,128)(2,1)S(1)}, u32[]{:S(2)}, u32[]{:S(2)}) collective-permute-start(bf16[8,96,768]{2,1,0:T(8,128)(2,1)S(1)} %collective-permute-done.7.rest_9_), channel_id=1, source_target_pairs={{0,4},{1,3},{2,6},{3,1},{4,0},{5,7},{6,2},{7,5}} | collective-permute-start | bytes 3538952 | tf_op jit(solution)/shard_map/ppermute | solution.py:63
  122.5 31.4 %collective-permute-start.16 = (bf16[6,96,768]{2,1,0:T(8,128)(2,1)}, bf16[6,96,768]{2,1,0:T(8,128)(2,1)S(1)}, u32[]{:S(2)}, u32[]{:S(2)}) collective-permute-start(bf16[6,96,768]{2,1,0:T(8,128)(2,1)} %collective-permute-done.14.rest_1_), channel_id=1, source_target_pairs={{0,4},{1,3},{2,6},{3,1},{4,0},{5,7},{6,2},{7,5}} | collective-permute-start | bytes 2654216 | tf_op jit(solution)/shard_map/ppermute | solution.py:63
  131.8 22.4 %collective-permute-start.18 = (bf16[6,96,768]{2,1,0:T(8,128)(2,1)}, bf16[6,96,768]{2,1,0:T(8,128)(2,1)S(1)}, u32[]{:S(2)}, u32[]{:S(2)}) collective-permute-start(bf16[6,96,768]{2,1,0:T(8,128)(2,1)} %collective-permute-done.14.rest_1_), channel_id=1, source_target_pairs={{0,1},{1,0},{2,3},{3,2},{4,5},{5,4},{6,7},{7,6}} | collective-permute-start | bytes 2654216 | tf_op jit(solution)/shard_map/ppermute | solution.py:63
  132.4 23.2 %collective-permute-start.19 = (bf16[6,96,768]{2,1,0:T(8,128)(2,1)}, bf16[6,96,768]{2,1,0:T(8,128)(2,1)S(1)}, u32[]{:S(2)}, u32[]{:S(2)}) collective-permute-start(bf16[6,96,768]{2,1,0:T(8,128)(2,1)} %collective-permute-done.15.rest_2_), channel_id=1, source_target_pairs={{0,1},{1,0},{2,3},{3,2},{4,5},{5,4},{6,7},{7,6}} | collective-permute-start | bytes 2654216 | tf_op jit(solution)/shard_map/ppermute | solution.py:63
  132.4 23.5 %collective-permute-start.11 = (bf16[8,96,768]{2,1,0:T(8,128)(2,1)S(1)}, bf16[8,96,768]{2,1,0:T(8,128)(2,1)S(1)}, u32[]{:S(2)}, u32[]{:S(2)}) collective-permute-start(bf16[8,96,768]{2,1,0:T(8,128)(2,1)S(1)} %collective-permute-done.7.rest_9_), channel_id=1, source_target_pairs={{0,1},{1,0},{2,3},{3,2},{4,5},{5,4},{6,7},{7,6}} | collective-permute-start | bytes 3538952 | tf_op jit(solution)/shard_map/ppermute | solution.py:63
  154.2 16.5 %collective-permute-start.23 = (bf16[8,96,768]{2,1,0:T(8,128)(2,1)}, bf16[8,96,768]{2,1,0:T(8,128)(2,1)}, u32[]{:S(2)}, u32[]{:S(2)}) collective-permute-start(bf16[8,96,768]{2,1,0:T(8,128)(2,1)} %collective-permute-done.21.rest_9_), channel_id=1, source_target_pairs={{0,4},{1,3},{2,6},{3,1},{4,0},{5,7},{6,2},{7,5}} | collective-permute-start | bytes 3538952 | tf_op jit(solution)/shard_map/ppermute | solution.py:63
  155.4 15.8 %collective-permute-start.13 = (bf16[8,96,768]{2,1,0:T(8,128)(2,1)S(1)}, bf16[8,96,768]{2,1,0:T(8,128)(2,1)S(1)}, u32[]{:S(2)}, u32[]{:S(2)}) collective-permute-start(bf16[8,96,768]{2,1,0:T(8,128)(2,1)S(1)} %collective-permute-done.9.rest_11_), channel_id=1, source_target_pairs={{0,1},{1,0},{2,3},{3,2},{4,5},{5,4},{6,7},{7,6}} | collective-permute-start | bytes 3538952 | tf_op jit(solution)/shard_map/ppermute | solution.py:63
  155.9 111.5 %collective-permute-start.24 = (bf16[8,96,768]{2,1,0:T(8,128)(2,1)S(1)}, bf16[8,96,768]{2,1,0:T(8,128)(2,1)}, u32[]{:S(2)}, u32[]{:S(2)}) collective-permute-start(bf16[8,96,768]{2,1,0:T(8,128)(2,1)S(1)} %pack.3.rest_8_), channel_id=1, source_target_pairs={{0,1},{1,0},{2,3},{3,2},{4,5},{5,4},{6,7},{7,6}} | collective-permute-start | bytes 3538952 | tf_op jit(solution)/shard_map/ppermute | solution.py:63
  156.7 110.7 %collective-permute-start.25 = (bf16[8,96,768]{2,1,0:T(8,128)(2,1)}, bf16[8,96,768]{2,1,0:T(8,128)(2,1)}, u32[]{:S(2)}, u32[]{:S(2)}) collective-permute-start(bf16[8,96,768]{2,1,0:T(8,128)(2,1)} %collective-permute-done.21.rest_9_), channel_id=1, source_target_pairs={{0,1},{1,0},{2,3},{3,2},{4,5},{5,4},{6,7},{7,6}} | collective-permute-start | bytes 3538952 | tf_op jit(solution)/shard_map/ppermute | solution.py:63
  170.7 96.7 %collective-permute-start.26 = (bf16[8,96,768]{2,1,0:T(8,128)(2,1)}, bf16[8,96,768]{2,1,0:T(8,128)(2,1)}, u32[]{:S(2)}, u32[]{:S(2)}) collective-permute-start(bf16[8,96,768]{2,1,0:T(8,128)(2,1)} %collective-permute-done.22.rest_10_), channel_id=1, source_target_pairs={{0,1},{1,0},{2,3},{3,2},{4,5},{5,4},{6,7},{7,6}} | collective-permute-start | bytes 3538952 | tf_op jit(solution)/shard_map/ppermute | solution.py:63
  170.8 96.7 %collective-permute-start.27 = (bf16[8,96,768]{2,1,0:T(8,128)(2,1)}, bf16[8,96,768]{2,1,0:T(8,128)(2,1)}, u32[]{:S(2)}, u32[]{:S(2)}) collective-permute-start(bf16[8,96,768]{2,1,0:T(8,128)(2,1)} %collective-permute-done.23.rest_11_), channel_id=1, source_target_pairs={{0,1},{1,0},{2,3},{3,2},{4,5},{5,4},{6,7},{7,6}} | collective-permute-start | bytes 3538952 | tf_op jit(solution)/shard_map/ppermute | solution.py:63
  172.8 52.5 %collective-permute-start.20 = (bf16[6,96,768]{2,1,0:T(8,128)(2,1)S(1)}, bf16[6,96,768]{2,1,0:T(8,128)(2,1)}, u32[]{:S(2)}, u32[]{:S(2)}) collective-permute-start(bf16[6,96,768]{2,1,0:T(8,128)(2,1)S(1)} %collective-permute-done.16.rest_3_), channel_id=1, source_target_pairs={{0,1},{1,0},{2,3},{3,2},{4,5},{5,4},{6,7},{7,6}} | collective-permute-start | bytes 2654216 | tf_op jit(solution)/shard_map/ppermute | solution.py:63
  (42 other events, 1120.8 us)

commit v2 on v1

--- a/solution.py
+++ b/solution.py
@@ -13,7 +13,6 @@
 BF16 = jnp.bfloat16
 ERF_SCALE = 0.7071067811865476
 SLOTS = 16
-NONE = {'transcendentals': 0}
 MIB = 2 ** 20
 
 
@@ -61,6 +60,7 @@
 def spread(shard):
     def hop(block, pairs):
         return lax.ppermute(block, 'fsdp', pairs)
+
     a = hop(shard, FIRST)
     b = hop(shard, SECOND)
     ab = hop(a, SECOND)
@@ -165,6 +165,7 @@
                                          device_id=(device,), device_id_type=MESH)
         c.start()
         return c
+
     def chips(at):
         c, cx, cy = at % 2, (at // 2) % 2, at // 4
         flip_x, flip_y = 1 - 2 * cx, 2 * (1 - 2 * cy)
@@ -172,6 +173,7 @@
         f = here + (1 - c) * flip_x + c * flip_y
         g = here + (1 - c) * flip_y + c * flip_x
         return here, g, f, f + g - here
+
     def held(block, dest, owner):
         parts = []
         for s in range(ids.shape[1]):
@@ -180,6 +182,7 @@
             tile = jnp.broadcast_to(here, (128, 128)).T.astype(BF16)
             parts.append(block[s * 128:(s + 1) * 128] * jnp.concatenate([tile] * (block.shape[1] // 128), axis=1))
         return jnp.concatenate(parts, axis=0)
+
     mine = chips(me)
     theirs = chips(pair)
     step = [send(j, src.at[theirs[j] * 2 + (1 - core)], r1.at[j], pair) for j in (2, 3, 1, 0)]
@@ -218,6 +221,7 @@
     def arrive(k, s, slot, device):
         pltpu.make_async_remote_copy(src_ref=out.at[slot, s], dst_ref=out.at[slot, s], send_sem=ssem.at[k, s], recv_sem=rsem.at[k, s],
                                      device_id=(device,), device_id_type=MESH).wait_recv()
+
     sent = []
     halves = range(src.shape[0])
     for s in halves:
@@ -260,6 +264,7 @@
         s0_ref[pl.ds(base, GROUP), :] = jnp.concatenate(rows0, axis=0)
         s1_ref[pl.ds(base, GROUP), :] = jnp.concatenate(rows1, axis=0)
         return carry
+
     lax.fori_loop(0, times // GROUP, trip, 0)
 
 
@@ -275,6 +280,7 @@
             if write is not None:
                 write(base + j, raw)
         return o0, o1
+
     return lax.fori_loop(0, times // GROUP, trip, init)
 
 
@@ -284,9 +290,30 @@
     return weights, jnp.sum(weights, axis=0, keepdims=True)
 
 
-def self_kernel(*refs):
-    for head in range(refs[1].shape[1]):
-        self_head(head, *refs)
+def self_kernel(layer, *refs):
+    heads_in, (h_ref, wide_ref), shards = refs[:6], refs[6:8], refs[8:16]
+    h_out, q_out, ko_ref, vo_ref, o, w, sems, s0_ref, s1_ref = refs[-9:]
+    step = pl.program_id(0)
+    per = heads_in[1].shape[1]
+
+    def loads(j):
+        return load_slot(shards, 3 + j, w.at[j], sems.at[j])
+
+    @pl.when(step == 0)
+    def _():
+        begin(loads(0) + loads(1))
+
+    for head in range(per):
+        self_head(head, *heads_in, o.at[pl.ds(step * per, per)], ko_ref, vo_ref, s0_ref, s1_ref)
+
+    @pl.when(step == pl.num_programs(0) - 1)
+    def _():
+        finish(loads(0) + loads(1))
+        h = h_ref[...] + (dot32(turn(o), w[0]) + bias_row(wide_ref, layer, 3))
+        h = norm_rows(h, *gain_row(wide_ref, layer, 0))
+        h_out[...] = h
+        q = (dot32(h.astype(BF16), w[1]) + bias_row(wide_ref, layer, 4)) * 0.125
+        q_out[...] = q.T.astype(BF16)
 
 
 def self_head(head, pos_ref, q_ref, kn_ref, vn_ref, k_ref, v_ref, *rest):
@@ -311,7 +338,9 @@
             for r in range(0, dim, pack):
                 rows = slice(r, r + pack)
                 out_ref[0, time, head, rows] = jnp.where(first, new0[rows], jnp.where(second, new1[rows], raw[rows]))
+
         return write
+
     scores_of(kc, q0, q1, s0_ref, s1_ref, times, writer(ko_ref, k0, k1))
     s00 = jnp.sum(q0 * k0.astype(F32), axis=0, keepdims=True)
     s10 = jnp.sum(q1 * k0.astype(F32), axis=0, keepdims=True)
@@ -333,9 +362,27 @@
     o_ref[head, :, lanes:] = (o1 / sum1).astype(BF16)
 
 
-def cross_kernel(*refs):
-    for head in range(refs[1].shape[0]):
-        cross_head(head, *refs)
+def cross_kernel(layer, *refs):
+    heads_in, (h_ref, wide_ref), shards = refs[:4], refs[4:6], refs[6:14]
+    h_out, o, w, sems, s0_ref, s1_ref = refs[14:]
+    step = pl.program_id(0)
+    per = heads_in[1].shape[0]
+
+    def loads():
+        return load_slot(shards, 5, w, sems)
+
+    @pl.when(step == 0)
+    def _():
+        begin(loads())
+
+    for head in range(per):
+        cross_head(head, *heads_in, o.at[pl.ds(step * per, per)], s0_ref, s1_ref)
+
+    @pl.when(step == pl.num_programs(0) - 1)
+    def _():
+        finish(loads())
+        h = h_ref[...] + (dot32(turn(o), w[...]) + bias_row(wide_ref, layer, 5))
+        h_out[...] = norm_rows(h, *gain_row(wide_ref, layer, 1))
 
 
 def cross_head(head, len_ref, q_ref, k_ref, v_ref, o_ref, s0_ref, s1_ref):
@@ -354,35 +401,19 @@
 
 
 def turn(o_ref):
-    return o_ref[...].astype(F32).T.astype(BF16)
-
-
-def mid_kernel(layer, h_ref, o_ref, wide_ref, *rest):
-    shards, (h_out, q_out, w, sems) = rest[:8], rest[8:]
-    loads = [begin(load_slot(shards, 3 + j, w.at[j], sems.at[j])) for j in range(2)]
-    o = turn(o_ref)
-    finish(loads[0])
-    h = h_ref[...] + (dot32(o, w[0]) + bias_row(wide_ref, layer, 3))
-    h = norm_rows(h, *gain_row(wide_ref, layer, 0))
-    h_out[...] = h
-    finish(loads[1])
-    q = (dot32(h.astype(BF16), w[1]) + bias_row(wide_ref, layer, 4)) * 0.125
-    q_out[...] = q.T.astype(BF16)
-
-
-def ffn_kernel(layer, h_ref, o_ref, wide_ref, *rest):
-    shards, inner_shards, (h_out, hb_out, w, up, down, sems) = rest[:8], rest[8:16], rest[16:]
-    part = shards[0].shape[1]
+    heads, dim, rows = o_ref.shape
+    return o_ref[...].reshape(heads * dim, rows).astype(F32).T.astype(BF16)
+
+
+def ffn_kernel(layer, h_ref, wide_ref, *rest):
+    inner_shards, (h_out, hb_out, up, down, sems) = rest[:8], rest[8:]
+    part = inner_shards[0].shape[1]
     width = h_ref.shape[1]
     blocks = up.shape[0]
-    first = begin(load_slot(shards, 5, w, sems.at[0]))
-    ups = [begin(load_slot(inner_shards, j, up.at[j], sems.at[1 + j])) for j in range(blocks)]
-    downs = begin([pltpu.make_async_copy(ref.at[pl.ds(blocks, blocks)], down.at[own], sems.at[1 + blocks, i])
+    ups = [begin(load_slot(inner_shards, j, up.at[j], sems.at[j])) for j in range(blocks)]
+    downs = begin([pltpu.make_async_copy(ref.at[pl.ds(blocks, blocks)], down.at[own], sems.at[blocks, i])
                    for i, (ref, own) in enumerate(zip(inner_shards, owners()))])
-    o = turn(o_ref)
-    finish(first)
-    h = h_ref[...] + (dot32(o, w[...]) + bias_row(wide_ref, layer, 5))
-    h = norm_rows(h, *gain_row(wide_ref, layer, 1))
+    h = h_ref[...]
     act = h.astype(BF16)
     acc = h + bias_row(wide_ref, layer, 12)
     per = width // (blocks * part)
@@ -414,6 +445,7 @@
     def _():
         for i in range(0, bias.shape[0], lanes):
             bias[i:i + lanes] = jnp.broadcast_to(bias_ref[0, :, i:i + lanes], (lanes, lanes)).T
+
     y = dot32(tok_ref[...], joined[step])
     for i in range(shards):
         cols = slice(i * lanes, (i + 1) * lanes)
@@ -431,6 +463,10 @@
     return pltpu.CompilerParams(vmem_limit_bytes=limit_mib * MIB, dimension_semantics=(sem,))
 
 
+def cost(flops):
+    return pl.CostEstimate(flops=flops, bytes_accessed=flops, transcendentals=0)
+
+
 def whole(shape):
     return pl.BlockSpec(shape, lambda i: (0,) * len(shape))
 
@@ -444,7 +480,7 @@
         in_specs=[pl.BlockSpec(memory_space=VM)] * 6, out_specs=[pl.BlockSpec(memory_space=VM)] * 2,
         scratch_shapes=[VM(shape, BF16) for shape in shapes[:5]] + [pltpu.SemaphoreType.DMA((6, 8)), pltpu.SemaphoreType.DMA((6, 8)), pltpu.SemaphoreType.DMA((6,))],
         compiler_params=pltpu.CompilerParams(collective_id=0, has_side_effects=True, vmem_limit_bytes=16 * MIB),
-        cost_estimate=pl.CostEstimate(flops=4000000, bytes_accessed=1000000, **NONE),
+        cost_estimate=cost(4000000),
     )(*srcs)
 
 
@@ -458,7 +494,7 @@
         scratch_shapes=[VM((4, rows, width), BF16), VM((4, rows, width), BF16), VM((2, rows, width), BF16), block, block,
                         pltpu.SemaphoreType.DMA((9,)), pltpu.SemaphoreType.DMA((9,))],
         compiler_params=pltpu.CompilerParams(collective_id=1, has_side_effects=True, vmem_limit_bytes=32 * MIB),
-        cost_estimate=pl.CostEstimate(flops=20000000, bytes_accessed=picked.size * 4, **NONE),
+        cost_estimate=cost(20000000),
     )(picked, ids, pos_rows, norm)
 
 
@@ -469,7 +505,7 @@
         in_specs=[pl.BlockSpec(memory_space=VM)], out_specs=pl.BlockSpec(memory_space=VM),
         scratch_shapes=[pltpu.SemaphoreType.DMA((7, rows.shape[0])), pltpu.SemaphoreType.DMA((7, rows.shape[0])), pltpu.SemaphoreType.DMA],
         compiler_params=pltpu.CompilerParams(collective_id=2, has_side_effects=True, vmem_limit_bytes=32 * MIB),
-        cost_estimate=pl.CostEstimate(flops=20000000, bytes_accessed=rows.size * 18, **NONE),
+        cost_estimate=cost(20000000),
     )(rows)
 
 
@@ -482,81 +518,63 @@
         out_specs=whole((3, width, rows)),
         scratch_shapes=[VM((3, width, width), BF16), pltpu.SemaphoreType.DMA((3, 8))],
         compiler_params=params(53),
-        cost_estimate=pl.CostEstimate(flops=2 * rows * width * width * 3, bytes_accessed=6 * width * width, **NONE),
+        cost_estimate=cost(2 * rows * width * width * 3),
     )(x, wide, *shards)
 
 
-def run_self(layer, pos, qkv, cache_k, cache_v, new_k, new_v, per=2):
+def run_self(layer, pos, qkv, cache_k, cache_v, new, h, shards, wide, per=2):
     _, times, heads, dim, lanes = cache_k.shape
-    rows = qkv.shape[-1]
+    rows, width = h.shape
     qkv = qkv.reshape(3, heads, dim, rows)
-    cache_spec = pl.BlockSpec((1, times, per, dim, lanes), lambda h: (layer, 0, h, 0, 0))
-    args = [pos, qkv, qkv, qkv, cache_k, cache_v]
-    specs = [whole((1, lanes))] + [pl.BlockSpec((1, per, dim, rows), functools.partial(lambda j, h: (j, h, 0, 0), j)) for j in range(3)]
-    specs += [cache_spec, cache_spec]
-    aliases = {}
-    if new_k is not None:
-        args += [new_k, new_v]
-        specs += [pl.BlockSpec(memory_space=pl.ANY)] * 2
-        aliases = {6: 1, 7: 2}
-    return pl.pallas_call(
-        self_kernel, grid=(heads // per,), name='self_attn',
-        out_shape=(jax.ShapeDtypeStruct((heads, dim, rows), BF16),
+    cache_spec = pl.BlockSpec((1, times, per, dim, lanes), lambda i: (layer, 0, i, 0, 0))
+    args = [pos, qkv, qkv, qkv, cache_k, cache_v, h, wide, *shards]
+    specs = [whole((1, lanes))] + [pl.BlockSpec((1, per, dim, rows), functools.partial(lambda j, i: (j, i, 0, 0), j)) for j in range(3)]
+    specs += [cache_spec, cache_spec, whole(h.shape), whole(wide.shape)] + [HBM] * len(shards)
+    aliases = {len(args) + i: 2 + i for i in range(len(new))}
+    return pl.pallas_call(
+        functools.partial(self_kernel, layer), grid=(heads // per,), name='self_attn',
+        out_shape=(jax.ShapeDtypeStruct(h.shape, F32), jax.ShapeDtypeStruct((width, rows), BF16),
                    jax.ShapeDtypeStruct(cache_k.shape, BF16), jax.ShapeDtypeStruct(cache_v.shape, BF16)),
-        in_specs=specs,
-        out_specs=(pl.BlockSpec((per, dim, rows), lambda h: (h, 0, 0)), cache_spec, cache_spec),
-        scratch_shapes=[VM((times, lanes), F32), VM((times, lanes), F32)],
+        in_specs=specs + [HBM] * len(new),
+        out_specs=(whole(h.shape), whole((width, rows)), cache_spec, cache_spec),
+        scratch_shapes=[VM((heads, dim, rows), BF16), VM((2, width, width), BF16), pltpu.SemaphoreType.DMA((2, 8)),
+                        VM((times, lanes), F32), VM((times, lanes), F32)],
         input_output_aliases=aliases,
-        compiler_params=params(53),
-        cost_estimate=pl.CostEstimate(flops=8 * heads * dim * rows * times, bytes_accessed=8 * times * heads * dim * lanes, **NONE),
-    )(*args)
-
-
-def run_cross(layer, lens, q, cross_k, cross_v, per=3):
+        compiler_params=params(53), cost_estimate=cost(8 * heads * dim * rows * times),
+    )(*args, *new)
+
+
+def run_cross(layer, lens, q, cross_k, cross_v, h, shards, wide, per=3):
     _, times, heads, dim, lanes = cross_k.shape
-    rows = q.shape[-1]
+    rows, width = h.shape
     q = q.reshape(heads, dim, rows)
-    spec = pl.BlockSpec((1, times, per, dim, lanes), lambda h: (layer, 0, h, 0, 0))
-    row_spec = pl.BlockSpec((per, dim, rows), lambda h: (h, 0, 0))
-    return pl.pallas_call(
-        cross_kernel, grid=(heads // per,), name='cross_attn',
-        out_shape=jax.ShapeDtypeStruct((heads, dim, rows), BF16),
-        in_specs=[whole((1, lanes)), row_spec, spec, spec],
-        out_specs=row_spec,
-        scratch_shapes=[VM((times, lanes), F32), VM((times, lanes), F32)],
-        compiler_params=params(53),
-        cost_estimate=pl.CostEstimate(flops=8 * heads * dim * rows * times, bytes_accessed=4 * times * heads * dim * lanes, **NONE),
-    )(lens, q, cross_k, cross_v)
-
-
-def run_mid(layer, h, o, shards, wide):
+    spec = pl.BlockSpec((1, times, per, dim, lanes), lambda i: (layer, 0, i, 0, 0))
+    return pl.pallas_call(
+        functools.partial(cross_kernel, layer), grid=(heads // per,), name='cross_attn',
+        out_shape=jax.ShapeDtypeStruct(h.shape, F32),
+        in_specs=[whole((1, lanes)), pl.BlockSpec((per, dim, rows), lambda i: (i, 0, 0)), spec, spec, whole(h.shape), whole(wide.shape)] + [HBM] * len(shards),
+        out_specs=whole(h.shape),
+        scratch_shapes=[VM((heads, dim, rows), BF16), VM((width, width), BF16), pltpu.SemaphoreType.DMA((8,)),
+                        VM((times, lanes), F32), VM((times, lanes), F32)],
+        compiler_params=params(53), cost_estimate=cost(8 * heads * dim * rows * times),
+    )(lens, q, cross_k, cross_v, h, wide, *shards)
+
+
+def run_ffn(layer, h, inner_shards, wide):
     rows, width = h.shape
-    return pl.pallas_call(
-        functools.partial(mid_kernel, layer), grid=(1,), name='mid',
-        out_shape=(jax.ShapeDtypeStruct((rows, width), F32), jax.ShapeDtypeStruct((width, rows), BF16)),
-        in_specs=[whole((rows, width)), whole((width, rows)), whole(wide.shape)] + [HBM] * 8,
-        out_specs=(whole((rows, width)), whole((width, rows))),
-        scratch_shapes=[VM((2, width, width), BF16), pltpu.SemaphoreType.DMA((2, 8))],
-        compiler_params=params(53),
-        cost_estimate=pl.CostEstimate(flops=4 * rows * width * width, bytes_accessed=4 * width * width, **NONE),
-    )(h, o.reshape(width, rows), wide, *shards)
-
-
-def run_ffn(layer, h, o, shards, inner_shards, wide):
-    rows, width = h.shape
-    part = shards[0].shape[1]
+    part = inner_shards[0].shape[1]
     blocks = inner_shards[0].shape[0] // 2
     inner = blocks * width
     return pl.pallas_call(
         functools.partial(ffn_kernel, layer), grid=(1,), name='ffn',
         out_shape=(jax.ShapeDtypeStruct((rows, width), F32), jax.ShapeDtypeStruct((2, width, rows // 2), BF16)),
-        in_specs=[whole((rows, width)), whole((width, rows)), whole(wide.shape)] + [HBM] * 16,
+        in_specs=[whole((rows, width)), whole(wide.shape)] + [HBM] * 8,
         out_specs=(whole((rows, width)), whole((2, width, rows // 2))),
-        scratch_shapes=[VM((width, width), BF16), VM((blocks, width, width), BF16), VM((8, blocks, part, width), BF16),
-                        pltpu.SemaphoreType.DMA((blocks + 2, 8))],
+        scratch_shapes=[VM((blocks, width, width), BF16), VM((8, blocks, part, width), BF16),
+                        pltpu.SemaphoreType.DMA((blocks + 1, 8))],
         compiler_params=params(53),
-        cost_estimate=pl.CostEstimate(flops=4 * rows * width * inner, bytes_accessed=4 * width * inner, **NONE),
-    )(h, o.reshape(width, rows), wide, *shards, *inner_shards)
+        cost_estimate=cost(4 * rows * width * inner),
+    )(h, wide, *inner_shards)
 
 
 def run_pack(layer, up, down):
@@ -568,7 +586,7 @@
         in_specs=[pl.BlockSpec((1, part, inner), lambda i: (layer, 0, 0)), pl.BlockSpec((1,) + down.shape[1:], lambda i: (layer, 0, 0))],
         out_specs=whole((2 * inner // width, part, width)),
         compiler_params=params(16),
-        cost_estimate=pl.CostEstimate(flops=2000000, bytes_accessed=8 * part * inner, **NONE),
+        cost_estimate=cost(2000000),
     )(up, down)
 
 
@@ -588,7 +606,7 @@
         out_specs=pl.BlockSpec((1, tile, rows), lambda v, s: (s, v, 0)),
         scratch_shapes=[VM((steps, width, rows), BF16), VM((bias.shape[2], lanes), F32)],
         compiler_params=pltpu.CompilerParams(vmem_limit_bytes=56 * MIB, dimension_semantics=('arbitrary', 'arbitrary')),
-        cost_estimate=pl.CostEstimate(flops=2 * steps * rows * vocab * width, bytes_accessed=4 * steps * rows * vocab, **NONE),
+        cost_estimate=cost(2 * steps * rows * vocab * width),
     )(hid, tok, bias)
 
 
@@ -621,9 +639,10 @@
         old_k, old_v, ck, cv = [c.transpose(to_lanes) for c in (self_k, self_v, cross_k, cross_v)]
         pos = positions[None, :]
         lens = src_len[None, :]
-        new_k = new_v = None
+        new = ()
         after = [wide, hidden]
-        attn = [attn_w[layer] for layer in range(layers)]
+        later, _ = lax.optimization_barrier((attn_w, picked))
+        attn = [attn_w[0]] + [later[layer] for layer in range(1, layers)]
         inner = [run_pack(layer, fc1_w, fc2_w) for layer in range(layers)]
         attn[0], _ = lax.optimization_barrier((attn[0], after[0]))
         inner[0], _ = lax.optimization_barrier((inner[0], after[1]))
@@ -632,13 +651,12 @@
         for layer in range(layers):
             w = attn_shards[layer]
             qkv = run_qkv(layer, hidden, w, wide)
-            o, new_k, new_v = run_self(layer, pos, qkv, old_k, old_v, new_k, new_v)
-            hidden, q = run_mid(layer, hidden, o, w, wide)
-            o = run_cross(layer, lens, q, ck, cv)
-            hidden, hidden_b = run_ffn(layer, hidden, o, w, inner_shards[layer], wide)
+            hidden, q, *new = run_self(layer, pos, qkv, old_k, old_v, new, hidden, w, wide)
+            hidden = run_cross(layer, lens, q, ck, cv, hidden, w, wide)
+            hidden, hidden_b = run_ffn(layer, hidden, inner_shards[layer], wide)
         rows = run_gather(hidden_b)
         logits = run_logits(rows, tok_embed, logit_bias)
         back = (0, 4, 1, 2, 3)
-        return logits.transpose(0, 2, 1), new_k.transpose(back), new_v.transpose(back)
+        return logits.transpose(0, 2, 1), *[z.transpose(back) for z in new]
 
     return jax.shard_map(decode, mesh=mesh, in_specs=in_specs, out_specs=out_specs, check_vma=False)

time: 330 us -> 328 us (level)
    unnamed x76 -> x70, local copies, waits for them, and re-layouts: 9.13 us -> 7.46 us
    pallas_call x6 -> x4, Pallas kernels: 73.3 us -> 72.2 us  [the longest x2 51 us: run_self(): pl.pallas_call(functools.partial(self_kernel, layer), grid=(heads // per,...]
  transfers between devices with their start and end apart: 28 -> 28, of which waited for: 7 -> 6; matrix products, arithmetic and copies ran while one was open for 5% -> 6% of each run, Pallas kernels for 38% -> 38%
where the time goes in v2:
time: 328 us; the launch traced here: 327 us
  Pallas kernels  190 us (58%)
  waiting for transfers between devices  90.2 us (28%)
  local copies, waits for them, and re-layouts  28.8 us (9%)
  starting transfers between devices  17 us (5%)
    ppermute x28, waiting for transfers between devices, hop(): return lax.ppermute(block, 'fsdp', pairs)  90.2 us
    pallas_call x2, Pallas kernels, run_self(): pl.pallas_call(functools.partial(self_kernel, layer), grid=(heads // per,...  51 us
    pallas_call x1, Pallas kernels, run_embed(): pl.pallas_call(functools.partial(embed_kernel, vocab), name='embed_sum',...  32.4 us
    pallas_call x1, Pallas kernels, run_logits(): pl.pallas_call(logits_kernel, grid=(tiles, steps), name='logits', out_sha...  31.1 us
    pallas_call x2, Pallas kernels, run_cross(): pl.pallas_call(functools.partial(cross_kernel, layer), grid=(heads // per...  21.2 us
    pallas_call x2, Pallas kernels, run_ffn(): pl.pallas_call(functools.partial(ffn_kernel, layer), grid=(1,), name='ffn...  19 us
    pallas_call x1, Pallas kernels, run_gather(): pl.pallas_call(gather_kernel, name='row_gather', out_shape=jax.ShapeDtype...  18.4 us
    ppermute x28, starting transfers between devices, hop(): return lax.ppermute(block, 'fsdp', pairs)  17 us
  transfers between devices with their start and end apart: 28, of which 6 were waited for; matrix products, arithmetic and copies ran while one was open for 6% of the time, Pallas kernels for 38%

profile of v2, /device:TPU:0, one launch (start us, length us, event | category | flops | bytes accessed | tf_op | source)
XLA Modules:
  0.0 327.2 jit_solution(16814363936191082856)
XLA Ops:
  0.7 2.2 slice_bitcast_fusion.1.rest_0_.refs_8_.refs_6_
  3.0 8.0 %small_gather.1 = (f32[40,768]{1,0:T(8,128)S(1)}, s32[16,2,128]{2,1,0:T(2,128)S(1)}) custom-call(bf16[6,2,96]{2,1,0:T(2,128)(2,1)S(1)} %bitcast.36, bf16[3,2,96]{2,1,0:T(2,128)(2,1)S(1)} %bitcast.37, bf16[3,2,96]{2,1,0:T(2,128)(2,1)S(1)} %bitcast.38, bf16[2,96]{1,0:T(2,128)(2,1)S(1)} %copy-done.20, bf16[2,384]{1,0:T(2,128)(2,1)S(1)} %copy-done.18, ...), custom_call_target="tpu_custom_call" | custom-call | flops 4000000 | bytes 4000000 | tf_op jit(solution)/shard_map/small_gather/pallas_call | solution.py:477
  13.9 15.0 %gather_fusion = bf16[2048,768]{1,0:T(8,128)(2,1)} fusion(bf16[6256,768]{1,0:T(8,128)(2,1)} %tok_ref.1, s32[2048]{0:T(1024)S(1)} %broadcast_clamp_fusion), kind=kCustom, calls=%fused_computation | custom fusion | bytes 6299648 | tf_op jit(solution)/shard_map/gather | solution.py:633
  28.9 2.2 slice_bitcast_fusion.rest_0_.refs_8_.refs_6_
  34.9 1.8 copy-done.2
  36.7 32.4 %embed_sum.1.x_ref.refs_6_ = f32[256,768]{1,0:T(8,128)S(1)} custom-call(bf16[8,256,768]{2,1,0:T(8,128)(2,1)S(1)} %bitcast.29, s32[16,2,128]{2,1,0:T(2,128)S(1)} %get-tuple-element.18.ids, bf16[256,768]{1,0:T(8,128)(2,1)S(1)} %gather_fusion.1, bf16[2,768]{1,0:T(2,128)(2,1)S(1)} %copy-done.12), custom_call_target="tpu_custom_call" | custom-call | flops 20000000 | bytes 20000000 | tf_op jit(solution)/shard_map/embed_sum/pallas_call | solution.py:490
  73.5 24.1 %collective-permute-done.7.rest_1_ = bf16[8,96,768]{2,1,0:T(8,128)(2,1)S(1)} collective-permute-done((bf16[8,96,768]{2,1,0:T(8,128)(2,1)S(1)}, bf16[8,96,768]{2,1,0:T(8,128)(2,1)S(1)}, u32[]{:S(2)}, u32[]{:S(2)}) %collective-permute-start.7) | collective-permute-done | bytes 1179680 | tf_op jit(solution)/shard_map/ppermute | solution.py:62
  97.6 1.8 collective-permute-start.2
  100.0 23.0 %collective-permute-done.21.rest_1_ = bf16[8,96,768]{2,1,0:T(8,128)(2,1)} collective-permute-done((bf16[8,96,768]{2,1,0:T(8,128)(2,1)S(1)}, bf16[8,96,768]{2,1,0:T(8,128)(2,1)}, u32[]{:S(2)}, u32[]{:S(2)}) %collective-permute-start.21) | collective-permute-done | bytes 1179680 | tf_op jit(solution)/shard_map/ppermute | solution.py:62
  123.0 1.8 collective-permute-start.16
  124.8 7.6 %collective-permute-done.2.rest_3_.refs_11_.refs_9_ = bf16[6,96,768]{2,1,0:T(8,128)(2,1)S(1)} collective-permute-done((bf16[6,96,768]{2,1,0:T(8,128)(2,1)}, bf16[6,96,768]{2,1,0:T(8,128)(2,1)S(1)}, u32[]{:S(2)}, u32[]{:S(2)}) %collective-permute-start.2) | collective-permute-done | bytes 884768 | tf_op jit(solution)/shard_map/ppermute | solution.py:62
  133.5 21.1 %collective-permute-done.16.rest_3_.refs_11_.refs_9_ = bf16[6,96,768]{2,1,0:T(8,128)(2,1)} collective-permute-done((bf16[6,96,768]{2,1,0:T(8,128)(2,1)}, bf16[6,96,768]{2,1,0:T(8,128)(2,1)}, u32[]{:S(2)}, u32[]{:S(2)}) %collective-permute-start.16) | collective-permute-done | bytes 884768 | tf_op jit(solution)/shard_map/ppermute | solution.py:62
  157.7 13.7 %collective-permute-done.23.rest_3_ = bf16[8,96,768]{2,1,0:T(8,128)(2,1)} collective-permute-done((bf16[8,96,768]{2,1,0:T(8,128)(2,1)}, bf16[8,96,768]{2,1,0:T(8,128)(2,1)}, u32[]{:S(2)}, u32[]{:S(2)}) %collective-permute-start.23) | collective-permute-done | bytes 1179680 | tf_op jit(solution)/shard_map/ppermute | solution.py:62
  174.7 4.4 %qkv.2 = bf16[3,768,256]{2,1,0:T(8,128)(2,1)} custom-call(f32[256,768]{1,0:T(8,128)S(1)} %embed_sum.1.x_ref.refs_6_, f32[40,768]{1,0:T(8,128)S(1)} %get-tuple-element.19.wide_ref.refs_7_.refs_5_, bf16[6,96,768]{2,1,0:T(8,128)(2,1)} %slice_bitcast_fusion.1.rest_0_.refs_8_.refs_6_, bf16[6,96,768]{2,1,0:T(8,128)(2,1)} %collective-permute-done.rest_1_.refs_9_.refs_7_, ...), custom_call_target="tpu_custom_call" | custom-call | flops 905969664 | bytes 905969664 | tf_op jit(solution)/shard_map/qkv/pallas_call | solution.py:514
  179.2 25.5 %self_attn.2 = (f32[256,768]{1,0:T(8,128)}, bf16[768,256]{1,0:T(8,128)(2,1)S(1)}, bf16[2,64,12,64,128]{4,3,2,1,0:T(8,128)(2,1)}, bf16[2,64,12,64,128]{4,3,2,1,0:T(8,128)(2,1)}) custom-call(s32[1,128]{1,0:T(1,128)S(1)} %bitcast.32, bf16[3,12,64,256]{3,2,1,0:T(8,128)(2,1)} %bitcast.53, bf16[3,12,64,256]{3,2,1,0:T(8,128)(2,1)} %bitcast.54, ...), custom_call_target="tpu_custom_call" | custom-call | flops 100663296 | bytes 100663296 | tf_op jit(solution)/shard_map/self_attn/pallas_call | solution.py:534
  204.7 10.6 %cross_attn.2.h_ref = f32[256,768]{1,0:T(8,128)} custom-call(s32[1,128]{1,0:T(1,128)S(1)} %bitcast.34, bf16[12,64,256]{2,1,0:T(8,128)(2,1)S(1)} %bitcast.31, bf16[2,32,12,64,128]{4,3,2,1,0:T(8,128)(2,1)} %bitcast.44, bf16[2,32,12,64,128]{4,3,2,1,0:T(8,128)(2,1)} %bitcast.46, f32[256,768]{1,0:T(8,128)} %get-tuple-element.22.refs_4_, ...), custom_call_target="tpu_custom_call" | custom-call | flops 50331648 | bytes 50331648 | tf_op jit(solution)/shard_map/cross_attn/pallas_call | solution.py:552
  215.3 9.5 %ffn.2 = (f32[256,768]{1,0:T(8,128)}, bf16[2,768,128]{2,1,0:T(8,128)(2,1)}) custom-call(f32[256,768]{1,0:T(8,128)} %cross_attn.2.h_ref, f32[40,768]{1,0:T(8,128)S(1)} %get-tuple-element.19.wide_ref.refs_7_.refs_5_, bf16[8,96,768]{2,1,0:T(8,128)(2,1)} %copy-done.5, bf16[8,96,768]{2,1,0:T(8,128)(2,1)} %copy-done.27, bf16[8,96,768]{2,1,0:T(8,128)(2,1)} %copy-done.28, ...), custom_call_target="tpu_custom_call" | custom-call | flops 2415919104 | bytes 2415919104 | tf_op jit(solution)/shard_map/ffn/pallas_call | solution.py:568
  226.0 4.4 %qkv.3 = bf16[3,768,256]{2,1,0:T(8,128)(2,1)} custom-call(f32[256,768]{1,0:T(8,128)S(1)} %copy-done.10, f32[40,768]{1,0:T(8,128)S(1)} %get-tuple-element.19.wide_ref.refs_7_.refs_5_, bf16[6,96,768]{2,1,0:T(8,128)(2,1)} %slice_bitcast_fusion.rest_0_.refs_8_.refs_6_, bf16[6,96,768]{2,1,0:T(8,128)(2,1)} %collective-permute-done.14.rest_1_.refs_9_.refs_7_, ...), custom_call_target="tpu_custom_call" | custom-call | flops 905969664 | bytes 905969664 | tf_op jit(solution)/shard_map/qkv/pallas_call | solution.py:514
  230.4 25.5 %self_attn.3 = (f32[256,768]{1,0:T(8,128)}, bf16[768,256]{1,0:T(8,128)(2,1)S(1)}, bf16[2,64,12,64,128]{4,3,2,1,0:T(8,128)(2,1)}, bf16[2,64,12,64,128]{4,3,2,1,0:T(8,128)(2,1)}) custom-call(s32[1,128]{1,0:T(1,128)S(1)} %bitcast.33, bf16[3,12,64,256]{3,2,1,0:T(8,128)(2,1)} %bitcast.50, ...), custom_call_target="tpu_custom_call", output_to_operand_aliasing={{2}: (16, {}), {3}: (17, {})} | custom-call | flops 100663296 | bytes 100663296 | tf_op jit(solution)/shard_map/self_attn/pallas_call | solution.py:534
  256.0 10.6 %cross_attn.3.h_ref = f32[256,768]{1,0:T(8,128)} custom-call(s32[1,128]{1,0:T(1,128)S(1)} %bitcast.35, bf16[12,64,256]{2,1,0:T(8,128)(2,1)S(1)} %bitcast.30, bf16[2,32,12,64,128]{4,3,2,1,0:T(8,128)(2,1)} %bitcast.45, bf16[2,32,12,64,128]{4,3,2,1,0:T(8,128)(2,1)} %bitcast.47, f32[256,768]{1,0:T(8,128)} %get-tuple-element.29.refs_4_, ...), custom_call_target="tpu_custom_call" | custom-call | flops 50331648 | bytes 50331648 | tf_op jit(solution)/shard_map/cross_attn/pallas_call | solution.py:552
  266.6 9.4 %ffn.3 = (f32[256,768]{1,0:T(8,128)}, bf16[2,768,128]{2,1,0:T(8,128)(2,1)S(1)}) custom-call(f32[256,768]{1,0:T(8,128)} %cross_attn.3.h_ref, f32[40,768]{1,0:T(8,128)S(1)} %get-tuple-element.19.wide_ref.refs_7_.refs_5_, bf16[8,96,768]{2,1,0:T(8,128)(2,1)} %copy-done.4, bf16[8,96,768]{2,1,0:T(8,128)(2,1)} %collective-permute-done.21.rest_1_, ...), custom_call_target="tpu_custom_call" | custom-call | flops 2415919104 | bytes 2415919104 | tf_op jit(solution)/shard_map/ffn/pallas_call | solution.py:568
  276.0 18.4 %row_gather.1.hid_ref = bf16[8,2,768,128]{3,2,1,0:T(8,128)(2,1)S(1)} custom-call(bf16[2,768,128]{2,1,0:T(8,128)(2,1)S(1)} %get-tuple-element.30.src), custom_call_target="tpu_custom_call" | custom-call | flops 20000000 | bytes 20000000 | tf_op jit(solution)/shard_map/row_gather/pallas_call | solution.py:502
  294.5 1.6 copy-done.11
  296.1 31.1 %logits.1 = f32[2,6256,1024]{2,1,0:T(8,128)} custom-call(bf16[8,2,768,128]{3,2,1,0:T(8,128)(2,1)} %copy-done.11, bf16[6256,768]{1,0:T(8,128)(2,1)} %tok_ref.1, f32[4,1,1664]{2,1,0:T(1,128)} %pad.9.bias_ref), custom_call_target="tpu_custom_call" | custom-call | flops 19679674368 | bytes 19679674368 | tf_op jit(solution)/shard_map/logits/pallas_call | solution.py:600
  (129 shorter events, 20.2 us)
Async XLA Ops:
  11.0 58.2 %collective-permute-start = (bf16[6,96,768]{2,1,0:T(8,128)(2,1)}, bf16[6,96,768]{2,1,0:T(8,128)(2,1)}, u32[]{:S(2)}, u32[]{:S(2)}) collective-permute-start(bf16[6,96,768]{2,1,0:T(8,128)(2,1)} %slice_bitcast_fusion.1.rest_0_.refs_8_.refs_6_), channel_id=1, source_target_pairs={{0,2},{1,5},{2,0},{3,7},{4,6},{5,1},{6,4},{7,3}} | collective-permute-start | bytes 2654216 | tf_op jit(solution)/shard_map/ppermute | solution.py:62
  12.4 56.8 %collective-permute-start.1 = (bf16[6,96,768]{2,1,0:T(8,128)(2,1)}, bf16[6,96,768]{2,1,0:T(8,128)(2,1)}, u32[]{:S(2)}, u32[]{:S(2)}) collective-permute-start(bf16[6,96,768]{2,1,0:T(8,128)(2,1)} %slice_bitcast_fusion.1.rest_0_.refs_8_.refs_6_), channel_id=1, source_target_pairs={{0,4},{1,3},{2,6},{3,1},{4,0},{5,7},{6,2},{7,5}} | collective-permute-start | bytes 2654216 | tf_op jit(solution)/shard_map/ppermute | solution.py:62
  13.9 55.9 %collective-permute-start.3 = (bf16[6,96,768]{2,1,0:T(8,128)(2,1)}, bf16[6,96,768]{2,1,0:T(8,128)(2,1)}, u32[]{:S(2)}, u32[]{:S(2)}) collective-permute-start(bf16[6,96,768]{2,1,0:T(8,128)(2,1)} %slice_bitcast_fusion.1.rest_0_.refs_8_.refs_6_), channel_id=1, source_target_pairs={{0,1},{1,0},{2,3},{3,2},{4,5},{5,4},{6,7},{7,6}} | collective-permute-start | bytes 2654216 | tf_op jit(solution)/shard_map/ppermute | solution.py:62
  31.1 40.0 %collective-permute-start.14 = (bf16[6,96,768]{2,1,0:T(8,128)(2,1)}, bf16[6,96,768]{2,1,0:T(8,128)(2,1)}, u32[]{:S(2)}, u32[]{:S(2)}) collective-permute-start(bf16[6,96,768]{2,1,0:T(8,128)(2,1)} %slice_bitcast_fusion.rest_0_.refs_8_.refs_6_), channel_id=1, source_target_pairs={{0,2},{1,5},{2,0},{3,7},{4,6},{5,1},{6,4},{7,3}} | collective-permute-start | bytes 2654216 | tf_op jit(solution)/shard_map/ppermute | solution.py:62
  31.7 39.5 %collective-permute-start.15 = (bf16[6,96,768]{2,1,0:T(8,128)(2,1)}, bf16[6,96,768]{2,1,0:T(8,128)(2,1)}, u32[]{:S(2)}, u32[]{:S(2)}) collective-permute-start(bf16[6,96,768]{2,1,0:T(8,128)(2,1)} %slice_bitcast_fusion.rest_0_.refs_8_.refs_6_), channel_id=1, source_target_pairs={{0,4},{1,3},{2,6},{3,1},{4,0},{5,7},{6,2},{7,5}} | collective-permute-start | bytes 2654216 | tf_op jit(solution)/shard_map/ppermute | solution.py:62
  69.2 28.4 %collective-permute-start.7 = (bf16[8,96,768]{2,1,0:T(8,128)(2,1)S(1)}, bf16[8,96,768]{2,1,0:T(8,128)(2,1)S(1)}, u32[]{:S(2)}, u32[]{:S(2)}) collective-permute-start(bf16[8,96,768]{2,1,0:T(8,128)(2,1)S(1)} %pack.2.rest_0_), channel_id=1, source_target_pairs={{0,2},{1,5},{2,0},{3,7},{4,6},{5,1},{6,4},{7,3}} | collective-permute-start | bytes 3538952 | tf_op jit(solution)/shard_map/ppermute | solution.py:62
  69.8 29.6 %collective-permute-start.8 = (bf16[8,96,768]{2,1,0:T(8,128)(2,1)S(1)}, bf16[8,96,768]{2,1,0:T(8,128)(2,1)S(1)}, u32[]{:S(2)}, u32[]{:S(2)}) collective-permute-start(bf16[8,96,768]{2,1,0:T(8,128)(2,1)S(1)} %pack.2.rest_0_), channel_id=1, source_target_pairs={{0,4},{1,3},{2,6},{3,1},{4,0},{5,7},{6,2},{7,5}} | collective-permute-start | bytes 3538952 | tf_op jit(solution)/shard_map/ppermute | solution.py:62
  71.1 28.3 %collective-permute-start.10 = (bf16[8,96,768]{2,1,0:T(8,128)(2,1)S(1)}, bf16[8,96,768]{2,1,0:T(8,128)(2,1)S(1)}, u32[]{:S(2)}, u32[]{:S(2)}) collective-permute-start(bf16[8,96,768]{2,1,0:T(8,128)(2,1)S(1)} %pack.2.rest_0_), channel_id=1, source_target_pairs={{0,1},{1,0},{2,3},{3,2},{4,5},{5,4},{6,7},{7,6}} | collective-permute-start | bytes 3538952 | tf_op jit(solution)/shard_map/ppermute | solution.py:62
  71.2 51.7 %collective-permute-start.21 = (bf16[8,96,768]{2,1,0:T(8,128)(2,1)S(1)}, bf16[8,96,768]{2,1,0:T(8,128)(2,1)}, u32[]{:S(2)}, u32[]{:S(2)}) collective-permute-start(bf16[8,96,768]{2,1,0:T(8,128)(2,1)S(1)} %pack.3.rest_0_), channel_id=1, source_target_pairs={{0,2},{1,5},{2,0},{3,7},{4,6},{5,1},{6,4},{7,3}} | collective-permute-start | bytes 3538952 | tf_op jit(solution)/shard_map/ppermute | solution.py:62
  72.7 50.2 %collective-permute-start.22 = (bf16[8,96,768]{2,1,0:T(8,128)(2,1)S(1)}, bf16[8,96,768]{2,1,0:T(8,128)(2,1)}, u32[]{:S(2)}, u32[]{:S(2)}) collective-permute-start(bf16[8,96,768]{2,1,0:T(8,128)(2,1)S(1)} %pack.3.rest_0_), channel_id=1, source_target_pairs={{0,4},{1,3},{2,6},{3,1},{4,0},{5,7},{6,2},{7,5}} | collective-permute-start | bytes 3538952 | tf_op jit(solution)/shard_map/ppermute | solution.py:62
  97.6 34.8 %collective-permute-start.2 = (bf16[6,96,768]{2,1,0:T(8,128)(2,1)}, bf16[6,96,768]{2,1,0:T(8,128)(2,1)S(1)}, u32[]{:S(2)}, u32[]{:S(2)}) collective-permute-start(bf16[6,96,768]{2,1,0:T(8,128)(2,1)} %collective-permute-done.rest_1_.refs_9_.refs_7_), channel_id=1, source_target_pairs={{0,4},{1,3},{2,6},{3,1},{4,0},{5,7},{6,2},{7,5}} | collective-permute-start | bytes 2654216 | tf_op jit(solution)/shard_map/ppermute | solution.py:62
  99.4 33.6 %collective-permute-start.4 = (bf16[6,96,768]{2,1,0:T(8,128)(2,1)}, bf16[6,96,768]{2,1,0:T(8,128)(2,1)}, u32[]{:S(2)}, u32[]{:S(2)}) collective-permute-start(bf16[6,96,768]{2,1,0:T(8,128)(2,1)} %collective-permute-done.rest_1_.refs_9_.refs_7_), channel_id=1, source_target_pairs={{0,1},{1,0},{2,3},{3,2},{4,5},{5,4},{6,7},{7,6}} | collective-permute-start | bytes 2654216 | tf_op jit(solution)/shard_map/ppermute | solution.py:62
  99.4 56.7 %collective-permute-start.9 = (bf16[8,96,768]{2,1,0:T(8,128)(2,1)S(1)}, bf16[8,96,768]{2,1,0:T(8,128)(2,1)S(1)}, u32[]{:S(2)}, u32[]{:S(2)}) collective-permute-start(bf16[8,96,768]{2,1,0:T(8,128)(2,1)S(1)} %collective-permute-done.7.rest_1_), channel_id=1, source_target_pairs={{0,4},{1,3},{2,6},{3,1},{4,0},{5,7},{6,2},{7,5}} | collective-permute-start | bytes 3538952 | tf_op jit(solution)/shard_map/ppermute | solution.py:62
  123.0 31.6 %collective-permute-start.16 = (bf16[6,96,768]{2,1,0:T(8,128)(2,1)}, bf16[6,96,768]{2,1,0:T(8,128)(2,1)}, u32[]{:S(2)}, u32[]{:S(2)}) collective-permute-start(bf16[6,96,768]{2,1,0:T(8,128)(2,1)} %collective-permute-done.14.rest_1_.refs_9_.refs_7_), channel_id=1, source_target_pairs={{0,4},{1,3},{2,6},{3,1},{4,0},{5,7},{6,2},{7,5}} | collective-permute-start | bytes 2654216 | tf_op jit(solution)/shard_map/ppermute | solution.py:62
  132.3 22.5 %collective-permute-start.18 = (bf16[6,96,768]{2,1,0:T(8,128)(2,1)}, bf16[6,96,768]{2,1,0:T(8,128)(2,1)S(1)}, u32[]{:S(2)}, u32[]{:S(2)}) collective-permute-start(bf16[6,96,768]{2,1,0:T(8,128)(2,1)} %collective-permute-done.14.rest_1_.refs_9_.refs_7_), channel_id=1, source_target_pairs={{0,1},{1,0},{2,3},{3,2},{4,5},{5,4},{6,7},{7,6}} | collective-permute-start | bytes 2654216 | tf_op jit(solution)/shard_map/ppermute | solution.py:62
  133.0 23.2 %collective-permute-start.19 = (bf16[6,96,768]{2,1,0:T(8,128)(2,1)}, bf16[6,96,768]{2,1,0:T(8,128)(2,1)S(1)}, u32[]{:S(2)}, u32[]{:S(2)}) collective-permute-start(bf16[6,96,768]{2,1,0:T(8,128)(2,1)} %collective-permute-done.15.rest_2_.refs_10_.refs_8_), channel_id=1, source_target_pairs={{0,1},{1,0},{2,3},{3,2},{4,5},{5,4},{6,7},{7,6}} | collective-permute-start | bytes 2654216 | tf_op jit(solution)/shard_map/ppermute | solution.py:62
  133.0 23.7 %collective-permute-start.11 = (bf16[8,96,768]{2,1,0:T(8,128)(2,1)S(1)}, bf16[8,96,768]{2,1,0:T(8,128)(2,1)S(1)}, u32[]{:S(2)}, u32[]{:S(2)}) collective-permute-start(bf16[8,96,768]{2,1,0:T(8,128)(2,1)S(1)} %collective-permute-done.7.rest_1_), channel_id=1, source_target_pairs={{0,1},{1,0},{2,3},{3,2},{4,5},{5,4},{6,7},{7,6}} | collective-permute-start | bytes 3538952 | tf_op jit(solution)/shard_map/ppermute | solution.py:62
  154.9 16.5 %collective-permute-start.23 = (bf16[8,96,768]{2,1,0:T(8,128)(2,1)}, bf16[8,96,768]{2,1,0:T(8,128)(2,1)}, u32[]{:S(2)}, u32[]{:S(2)}) collective-permute-start(bf16[8,96,768]{2,1,0:T(8,128)(2,1)} %collective-permute-done.21.rest_1_), channel_id=1, source_target_pairs={{0,4},{1,3},{2,6},{3,1},{4,0},{5,7},{6,2},{7,5}} | collective-permute-start | bytes 3538952 | tf_op jit(solution)/shard_map/ppermute | solution.py:62
  156.1 15.8 %collective-permute-start.13 = (bf16[8,96,768]{2,1,0:T(8,128)(2,1)S(1)}, bf16[8,96,768]{2,1,0:T(8,128)(2,1)S(1)}, u32[]{:S(2)}, u32[]{:S(2)}) collective-permute-start(bf16[8,96,768]{2,1,0:T(8,128)(2,1)S(1)} %collective-permute-done.9.rest_3_), channel_id=1, source_target_pairs={{0,1},{1,0},{2,3},{3,2},{4,5},{5,4},{6,7},{7,6}} | collective-permute-start | bytes 3538952 | tf_op jit(solution)/shard_map/ppermute | solution.py:62
  156.7 109.9 %collective-permute-start.24 = (bf16[8,96,768]{2,1,0:T(8,128)(2,1)S(1)}, bf16[8,96,768]{2,1,0:T(8,128)(2,1)}, u32[]{:S(2)}, u32[]{:S(2)}) collective-permute-start(bf16[8,96,768]{2,1,0:T(8,128)(2,1)S(1)} %pack.3.rest_0_), channel_id=1, source_target_pairs={{0,1},{1,0},{2,3},{3,2},{4,5},{5,4},{6,7},{7,6}} | collective-permute-start | bytes 3538952 | tf_op jit(solution)/shard_map/ppermute | solution.py:62
  157.4 109.2 %collective-permute-start.25 = (bf16[8,96,768]{2,1,0:T(8,128)(2,1)}, bf16[8,96,768]{2,1,0:T(8,128)(2,1)}, u32[]{:S(2)}, u32[]{:S(2)}) collective-permute-start(bf16[8,96,768]{2,1,0:T(8,128)(2,1)} %collective-permute-done.21.rest_1_), channel_id=1, source_target_pairs={{0,1},{1,0},{2,3},{3,2},{4,5},{5,4},{6,7},{7,6}} | collective-permute-start | bytes 3538952 | tf_op jit(solution)/shard_map/ppermute | solution.py:62
  171.4 95.2 %collective-permute-start.26 = (bf16[8,96,768]{2,1,0:T(8,128)(2,1)}, bf16[8,96,768]{2,1,0:T(8,128)(2,1)}, u32[]{:S(2)}, u32[]{:S(2)}) collective-permute-start(bf16[8,96,768]{2,1,0:T(8,128)(2,1)} %collective-permute-done.22.rest_2_), channel_id=1, source_target_pairs={{0,1},{1,0},{2,3},{3,2},{4,5},{5,4},{6,7},{7,6}} | collective-permute-start | bytes 3538952 | tf_op jit(solution)/shard_map/ppermute | solution.py:62
  171.4 95.2 %collective-permute-start.27 = (bf16[8,96,768]{2,1,0:T(8,128)(2,1)}, bf16[8,96,768]{2,1,0:T(8,128)(2,1)}, u32[]{:S(2)}, u32[]{:S(2)}) collective-permute-start(bf16[8,96,768]{2,1,0:T(8,128)(2,1)} %collective-permute-done.23.rest_3_), channel_id=1, source_target_pairs={{0,1},{1,0},{2,3},{3,2},{4,5},{5,4},{6,7},{7,6}} | collective-permute-start | bytes 3538952 | tf_op jit(solution)/shard_map/ppermute | solution.py:62
  173.4 51.4 %collective-permute-start.20 = (bf16[6,96,768]{2,1,0:T(8,128)(2,1)}, bf16[6,96,768]{2,1,0:T(8,128)(2,1)}, u32[]{:S(2)}, u32[]{:S(2)}) collective-permute-start(bf16[6,96,768]{2,1,0:T(8,128)(2,1)} %collective-permute-done.16.rest_3_.refs_11_.refs_9_), channel_id=1, source_target_pairs={{0,1},{1,0},{2,3},{3,2},{4,5},{5,4},{6,7},{7,6}} | collective-permute-start | bytes 2654216 | tf_op jit(solution)/shard_map/ppermute | solution.py:62
  (39 other events, 1005.0 us)
